TPU v7x, 128 devices: a whole 4x4x4 slice. The times are simulated.
128 devices in a mesh: dp: 8 (over x, core), mp: 16 (over z, y).
Axes of the slice: x: 4, y: 4, z: 4, core: 2. Of those that a mesh axis runs over, the one named last changes fastest.
Arguments:
- tokens: bfloat16 [2048, 8192], P('dp'), may hold values from -6 to 6
- norm_gain: float32 [8192], replicated, may hold values from 0.5 to 1.5
- gate_weight: bfloat16 [8192, 28672], P('dp', 'mp'), may hold values from -0.0625 to 0.0625
- gate_mask: int32 [8192, 896], P('dp', 'mp'), may hold values from -2147483648 to 2147483646
- up_weight: bfloat16 [8192, 28672], P('dp', 'mp'), may hold values from -0.0625 to 0.0625
- up_mask: int32 [8192, 896], P('dp', 'mp'), may hold values from -2147483648 to 2147483646
- down_weight: bfloat16 [28672, 8192], P('mp', 'dp'), may hold values from -0.03125 to 0.03125
- down_mask: int32 [28672, 256], P('mp', 'dp'), may hold values from -2147483648 to 2147483647, as said below
Outputs:
- mixed: bfloat16 [2048, 8192], P('mp', 'dp')
- input_norms: float32 [8192], P('dp')
- hidden_norms: float32 [28672], P('mp')
Inputs may be any that keep to these rules, and one draw needn't show every extreme that they name: `down_mask`: in every word each of the eight aligned groups of four bits holds exactly two ones, so exactly two of every four consecutive columns of the down projection are kept.
All inputs are finite; a program needn't handle non-finite values.
Results may differ from a plain program's by a relative error of at most 0.025.
Values may be sent and summed in bfloat16 or wider, within the bound.
A program may use at most 128 MiB of HBM per device.

v0:
```python
import jax
import jax.numpy as jnp
from jax import lax
from jax.sharding import Mesh
from jax.sharding import PartitionSpec as P

MP = ("mp_0", "mp_1")


def sent_to_all(array, axis):
    length = lax.axis_size(axis)
    return lax.all_to_all(
        jnp.broadcast_to(array[None], (length, *array.shape)), axis, 0, 0, tiled=True
    )


def over_copies(array, axis):
    return sent_to_all(array, axis).sum(axis=0)


def sum_by_axis(array, axes, dim):
    for axis in axes:
        array = lax.psum_scatter(array, axis, scatter_dimension=dim, tiled=True)
    return array


def keep_entries(weight, packed):
    shifts = jnp.arange(32, dtype=jnp.int32)
    kept_bits = jnp.right_shift(packed[..., None], shifts) & 1
    kept_bits = kept_bits.reshape(weight.shape)
    return jnp.where(kept_bits == 1, weight, jnp.zeros_like(weight))


def on_device(
    tokens, norm_gain, gate_weight, gate_mask, up_weight, up_mask, down_weight, down_mask
):
    values = tokens.astype(jnp.float32)
    scale = lax.rsqrt(jnp.mean(values * values, axis=1, keepdims=True) + 1e-05)
    normed = (values * scale * norm_gain).astype(jnp.bfloat16)
    columns = lax.all_to_all(normed, "dp", split_axis=1, concat_axis=0, tiled=True)
    widened = columns.astype(jnp.float32)
    input_norms = jnp.sqrt(jnp.sum(widened * widened, axis=0))
    gate_kept = keep_entries(gate_weight, gate_mask)
    up_kept = keep_entries(up_weight, up_mask)
    down_kept = keep_entries(down_weight, down_mask)
    units = gate_kept.shape[1]
    gate_part = jnp.dot(columns, gate_kept, preferred_element_type=jnp.float32)
    up_part = jnp.dot(columns, up_kept, preferred_element_type=jnp.float32)
    both_sums = lax.psum_scatter(
        jnp.concatenate([gate_part, up_part], axis=1).astype(jnp.bfloat16),
        "dp",
        scatter_dimension=0,
        tiled=True,
    ).astype(jnp.float32)
    hidden = (jax.nn.silu(both_sums[:, :units]) * both_sums[:, units:]).astype(jnp.bfloat16)
    wide_hidden = hidden.astype(jnp.float32)
    squares = over_copies(jnp.sum(wide_hidden * wide_hidden, axis=0), "dp")
    hidden_norms = jnp.sqrt(squares)
    partial_out = jnp.dot(
        lax.all_gather(hidden, "dp", axis=0, tiled=True),
        down_kept,
        preferred_element_type=jnp.float32,
    )
    mixed = (
        sum_by_axis(partial_out.astype(jnp.bfloat16), MP, 0)
        .astype(jnp.float32)
        .astype(jnp.bfloat16)
    )
    return (mixed, input_norms, hidden_norms)


def solution(mesh):
    finer = Mesh(mesh.devices.reshape(mesh.shape["dp"], 4, 4), ("dp", "mp_0", "mp_1"))
    in_specs = (
        P("dp", None),
        P(),
        P("dp", MP),
        P("dp", MP),
        P("dp", MP),
        P("dp", MP),
        P(MP, "dp"),
        P(MP, "dp"),
    )
    out_specs = (P(MP, "dp"), P("dp"), P(MP))
    return jax.shard_map(
        on_device, mesh=finer, in_specs=in_specs, out_specs=out_specs, check_vma=False
    )
```

profile of v0, /device:TPU:0, one launch (start us, length us, event | category | flops | bytes accessed | tf_op | source)
XLA Modules:
  0.0 346.1 jit_solution(16962766649375081931)
XLA Ops:
  7.2 6.4 %copy.27 = bf16[256,8192]{0,1:T(8,128)(2,1)} copy(bf16[256,8192]{1,0:T(8,128)(2,1)} %param.8) | data formatting | bytes 8388608 | tf_op args[0]
  13.5 3.5 fusion
  17.0 2.6 fusion.2
  19.7 4.6 %all-to-all-start = ((bf16[256,8,1024]{0,2,1:T(8,128)(2,1)}), bf16[256,8,1024]{0,2,1:T(8,128)(2,1)}, u32[]{:S(2)}, u32[]{:S(2)}) async-start(bf16[256,8,1024]{0,2,1:T(8,128)(2,1)} %bitcast.34), calls=%async_computation | async-start | bytes 8388608 | tf_op jit(solution)/shard_map/all_to_all | solution.py:40
  24.5 6.0 %copy.29 = bf16[1024,1792]{0,1:T(8,128)(2,1)} copy(bf16[1024,1792]{1,0:T(8,128)(2,1)} %param.10) | data formatting | bytes 7340032 | tf_op args[2]
  30.5 6.0 %copy.30 = bf16[1024,1792]{0,1:T(8,128)(2,1)} copy(bf16[1024,1792]{1,0:T(8,128)(2,1)} %param.12) | data formatting | bytes 7340032 | tf_op args[4]
  36.5 6.7 %fusion.9 = (bf16[1024,1792]{0,1:T(8,128)(2,1)}, bf16[1024,1792]{0,1:T(8,128)(2,1)}) fusion(bf16[1024,1792]{0,1:T(8,128)(2,1)} %copy.29, s32[1792]{0:T(1024)S(1)} %shift_right_arithmetic.63, s32[1024,56]{0,1:T(8,128)S(1)} %copy-done.3, bf16[1024,1792]{0,1:T(8,128)(2,1)} %copy.30, s32[1024,56]{0,1:T(8,128)S(1)} %copy-done.4), kind=kLoop, calls=%fused_computation.18 | loop fusion | flops 14680064 | bytes 15145984 | tf_op jit(solution)/shard_map/jit(_where)/select_n | solution.py:31
  43.2 30.6 %all-to-all-done = bf16[256,8,1024]{0,2,1:T(8,128)(2,1)} async-done(((bf16[256,8,1024]{0,2,1:T(8,128)(2,1)}), bf16[256,8,1024]{0,2,1:T(8,128)(2,1)}, u32[]{:S(2)}, u32[]{:S(2)}) %all-to-all-start) | async-done | bytes 4194336 | tf_op jit(solution)/shard_map/all_to_all | solution.py:40
  73.9 6.5 %copy.28 = bf16[8,256,1024]{2,1,0:T(8,128)(2,1)} copy(bf16[8,256,1024]{1,2,0:T(8,128)(2,1)} %bitcast.1) | data formatting | bytes 8388608 | tf_op jit(solution)/shard_map/all_to_all | solution.py:40
  80.3 10.9 %convolution_convert_fusion = bf16[2048,1792]{0,1:T(8,128)(2,1)S(1)} fusion(bf16[2048,1024]{1,0:T(8,128)(2,1)} %bitcast.35, bf16[1024,1792]{0,1:T(8,128)(2,1)} %get-tuple-element.6), kind=kOutput, calls=%fused_computation.7 | convolution fusion | flops 7519862784 | bytes 15204352 | tf_op jit(solution)/shard_map/dot_general | solution.py:48
  91.3 8.4 %convolution_convert_fusion.1 = bf16[2048,1792]{0,1:T(8,128)(2,1)S(1)} fusion(bf16[2048,1024]{1,0:T(8,128)(2,1)S(1)} %bitcast.36, bf16[1024,1792]{0,1:T(8,128)(2,1)S(1)} %copy-done.2), kind=kOutput, calls=%fused_computation.8 | convolution fusion | flops 7519862784 | bytes 15204352 | tf_op jit(solution)/shard_map/dot_general | solution.py:47
  99.7 17.1 %pad_maximum_fusion = bf16[2048,3584]{0,1:T(8,128)(2,1)} fusion(bf16[2048,1792]{0,1:T(8,128)(2,1)S(1)} %convolution_convert_fusion, bf16[2048,1792]{0,1:T(8,128)(2,1)S(1)} %convolution_convert_fusion.1), kind=kLoop, calls=%fused_computation | loop fusion | flops 29360128 | bytes 29360128 | tf_op jit(solution)/shard_map/concatenate | solution.py:50
  116.9 83.1 %reduce-scatter.4.cloned.1.call-done = bf16[256,3584]{0,1:T(8,128)(2,1)} async-done(((bf16[2048,3584]{0,1:T(8,128)(2,1)}), bf16[256,3584]{0,1:T(8,128)(2,1)}) %reduce-scatter.4.cloned.1.call-update) | async-done | bytes 1835024 | tf_op jit(solution)/shard_map/reduce_scatter | solution.py:49
  199.9 1.8 convert_element_type.27
  201.7 1.5 multiply_reduce_fusion.1
  203.6 5.9 %copy.31 = bf16[1792,1024]{0,1:T(8,128)(2,1)} copy(bf16[1792,1024]{1,0:T(8,128)(2,1)} %param.14) | data formatting | bytes 7340032 | tf_op args[6]
  209.5 4.5 %fusion.11 = bf16[1792,1024]{0,1:T(8,128)(2,1)} fusion(bf16[1792,1024]{0,1:T(8,128)(2,1)} %copy.31, s32[1024]{0:T(1024)S(1)} %shift_right_arithmetic.72, s32[1792,32]{0,1:T(8,128)S(1)} %copy-done.5), kind=kLoop, calls=%fused_computation.20 | loop fusion | flops 7340032 | bytes 7573504 | tf_op jit(solution)/shard_map/jit(_where)/select_n | solution.py:31
  214.0 37.9 %all-gather.2.cloned.1.call-done = bf16[2048,1792]{0,1:T(8,128)(2,1)} async-done(((bf16[256,1792]{0,1:T(8,128)(2,1)}), bf16[2048,1792]{0,1:T(8,128)(2,1)}) %all-gather.2.cloned.1.call-update) | async-done | bytes 7340048 | tf_op jit(solution)/shard_map/all_gather | solution.py:60
  251.9 13.2 %convolution_convert_fusion.2 = bf16[2048,1024]{1,0:T(8,128)(2,1)} fusion(bf16[2048,1792]{0,1:T(8,128)(2,1)} %all-gather.2.cloned.1.call-done, bf16[1792,1024]{0,1:T(8,128)(2,1)} %fusion.11), kind=kOutput, calls=%fused_computation.21 | convolution fusion | flops 7518289920 | bytes 15204352 | tf_op jit(solution)/shard_map/dot_general | solution.py:59
  265.2 48.1 %reduce-scatter.6.cloned.1.call-done = bf16[512,1024]{1,0:T(8,128)(2,1)} async-done(((bf16[2048,1024]{1,0:T(8,128)(2,1)}), bf16[512,1024]{1,0:T(8,128)(2,1)}) %reduce-scatter.6.cloned.1.call-update) | async-done | bytes 1048592 | tf_op jit(solution)/shard_map/reduce_scatter | solution.py:23
  314.0 4.3 %all-to-all-start.1 = ((f32[8,1,1792]{2,1,0:T(1,128)}), f32[8,1,1792]{2,1,0:T(1,128)S(1)}, u32[]{:S(2)}, u32[]{:S(2)}) async-start(f32[8,1,1792]{2,1,0:T(1,128)} %broadcast_in_dim.5), calls=%async_computation.4 | async-start | bytes 114688 | tf_op jit(solution)/shard_map/all_to_all | solution.py:12
  318.3 3.1 multiply_reduce_fusion
  321.9 1.9 all-to-all-done.1
  324.5 15.1 %reduce-scatter.8.cloned.1.call-done = bf16[128,1024]{1,0:T(8,128)(2,1)} async-done(((bf16[512,1024]{1,0:T(8,128)(2,1)}), bf16[128,1024]{1,0:T(8,128)(2,1)}) %reduce-scatter.8.cloned.1.call-update) | async-done | bytes 262160 | tf_op jit(solution)/shard_map/reduce_scatter | solution.py:23
  (31 shorter events, 2.7 us)
Async XLA Ops:
  7.2 9.8 %copy-start.6 = (f32[8192]{0:T(1024)S(1)}, f32[8192]{0:T(1024)}, u32[]{:S(2)}) copy-start(f32[8192]{0:T(1024)} %param.9) | copy-start | bytes 98308
  13.5 3.5 %copy-start = (bf16[256,8192]{0,1:T(8,128)(2,1)S(1)}, bf16[256,8192]{0,1:T(8,128)(2,1)}, u32[]{:S(2)}) copy-start(bf16[256,8192]{0,1:T(8,128)(2,1)} %copy.27) | copy-start | bytes 12582916
  19.7 54.2 %all-to-all-start = ((bf16[256,8,1024]{0,2,1:T(8,128)(2,1)}), bf16[256,8,1024]{0,2,1:T(8,128)(2,1)}, u32[]{:S(2)}, u32[]{:S(2)}) async-start(bf16[256,8,1024]{0,2,1:T(8,128)(2,1)} %bitcast.34), calls=%async_computation | async-start | bytes 8388608 | tf_op jit(solution)/shard_map/all_to_all | solution.py:40
  24.2 175.7 %reduce-scatter.4.cloned.1.call-start = ((), (), s32[]{:S(2)}) async-start(), calls=%async_computation.5 | async-start | bytes 16515072 | tf_op jit(solution)/shard_map/reduce_scatter | solution.py:49
  30.5 6.0 %copy-start.3 = (s32[1024,56]{0,1:T(8,128)S(1)}, s32[1024,56]{0,1:T(8,128)}, u32[]{:S(2)}) copy-start(s32[1024,56]{0,1:T(8,128)} %param.11) | copy-start | bytes 688132
  30.5 6.0 %copy-start.4 = (s32[1024,56]{0,1:T(8,128)S(1)}, s32[1024,56]{0,1:T(8,128)}, u32[]{:S(2)}) copy-start(s32[1024,56]{0,1:T(8,128)} %param.13) | copy-start | bytes 688132
  80.3 10.9 %copy-start.1 = (bf16[8,256,1024]{2,1,0:T(8,128)(2,1)S(1)}, bf16[8,256,1024]{2,1,0:T(8,128)(2,1)}, u32[]{:S(2)}) copy-start(bf16[8,256,1024]{2,1,0:T(8,128)(2,1)} %copy.28) | copy-start | bytes 12582916
  80.3 10.9 %copy-start.2 = (bf16[1024,1792]{0,1:T(8,128)(2,1)S(1)}, bf16[1024,1792]{0,1:T(8,128)(2,1)}, u32[]{:S(2)}) copy-start(bf16[1024,1792]{0,1:T(8,128)(2,1)} %get-tuple-element.5) | copy-start | bytes 11010052
  116.8 135.1 %all-gather.2.cloned.1.call-start = ((), (), s32[]{:S(2)}) async-start(), calls=%async_computation.6 | async-start | bytes 8257536 | tf_op jit(solution)/shard_map/all_gather | solution.py:60
  203.2 6.3 %copy-start.5 = (s32[1792,32]{0,1:T(8,128)S(1)}, s32[1792,32]{0,1:T(8,128)}, u32[]{:S(2)}) copy-start(s32[1792,32]{0,1:T(8,128)} %param.15) | copy-start | bytes 688132
  203.3 110.1 %reduce-scatter.6.cloned.1.call-start = ((), (), s32[]{:S(2)}) async-start(), calls=%async_computation.7 | async-start | bytes 5242880 | tf_op jit(solution)/shard_map/reduce_scatter | solution.py:23
  265.2 74.4 %reduce-scatter.8.cloned.1.call-start = ((), (), s32[]{:S(2)}) async-start(), calls=%async_computation.8 | async-start | bytes 1310720 | tf_op jit(solution)/shard_map/reduce_scatter | solution.py:23
  314.0 9.8 %all-to-all-start.1 = ((f32[8,1,1792]{2,1,0:T(1,128)}), f32[8,1,1792]{2,1,0:T(1,128)S(1)}, u32[]{:S(2)}, u32[]{:S(2)}) async-start(f32[8,1,1792]{2,1,0:T(1,128)} %broadcast_in_dim.5), calls=%async_computation.4 | async-start | bytes 114688 | tf_op jit(solution)/shard_map/all_to_all | solution.py:12
Sparse Core Ops, SparseCore 0:
  116.9 82.9 reduce-scatter.3
  203.4 48.4 all-gather.1
  265.3 48.0 reduce-scatter.5
  316.2 23.3 reduce-scatter.7
where the time goes:
time: 347 us; the launch traced here: 346 us
  waiting for transfers between devices  217 us (63%)
  other arithmetic  40.8 us (12%)
  local copies, waits for them, and re-layouts  32.7 us (9%)
  matrix products  32.5 us (9%)
  between operations  13.9 us (4%)
  starting transfers between devices  9.37 us (3%)
    reduce_scatter x1, waiting for transfers between devices, on_device(): lax.psum_scatter(jnp.concatenate([gate_part, up_part], axis=1).astype(jnp...  83.1 us
    reduce_scatter x2, waiting for transfers between devices, sum_by_axis(): array = lax.psum_scatter(array, axis, scatter_dimension=dim, tiled=True)  63.2 us
    all_gather x1, waiting for transfers between devices, on_device(): lax.all_gather(hidden, 'dp', axis=0, tiled=True)  37.9 us
    all_to_all x1, waiting for transfers between devices, on_device(): lax.all_to_all(normed, 'dp', split_axis=1, concat_axis=0, tiled=True)  30.6 us
    unnamed x18, local copies, waits for them, and re-layouts  24.2 us
    concatenate x1, other arithmetic, on_device(): jnp.concatenate([gate_part, up_part], axis=1).astype(jnp.bfloat16)  17.1 us
    dot_general x1, matrix products, on_device(): jnp.dot(lax.all_gather(hidden, 'dp', axis=0, tiled=True), down_kept, pref...  13.2 us
    select_n x2, other arithmetic, keep_entries(): return jnp.where(kept_bits == 1, weight, jnp.zeros_like(weight))  11.2 us
  transfers between devices with their start and end apart: 6, of which 6 were waited for; matrix products, arithmetic and copies ran while one was open for 10% of the time, Pallas kernels for 0%

commit v1 on v0

v1 whole, which is shorter than its diff:
```python
import functools

import jax
import jax.numpy as jnp
from jax import lax
from jax.experimental import pallas as pl
from jax.experimental.pallas import tpu as pltpu
from jax.sharding import PartitionSpec as P

MESH = pl.DeviceIdType.MESH
BF = jnp.bfloat16
F32 = jnp.float32

NX = 4
G = 4
RT = 256
R = RT // G
H = R // 2
NT = 7
FC = 2048
UH = 896


def norm_kernel(tok_ref, gain_ref, out_ref):
    v = tok_ref[...].astype(F32)
    scale = lax.rsqrt(jnp.sum(v * v, axis=1, keepdims=True) * (1.0 / 8192) + 1e-05)
    n = (v * scale * gain_ref[...]).astype(BF)
    for i in range(NX):
        out_ref[i] = n[:, i * FC : (i + 1) * FC]


def norm_call(tokens, gain):
    return pl.pallas_call(
        norm_kernel,
        grid=(2 * G,),
        in_specs=[
            pl.BlockSpec((H, 8192), lambda b: (b, 0)),
            pl.BlockSpec((1, 8192), lambda b: (0, 0)),
        ],
        out_specs=pl.BlockSpec((NX, H, FC), lambda b: (0, (b % G) * 2 + b // G, 0)),
        out_shape=jax.ShapeDtypeStruct((NX, RT, FC), BF),
    )(tokens, gain.reshape(1, 8192))


def kept(words, weight, tile):
    lane = lax.broadcasted_iota(jnp.int32, words.shape, 1)
    spread = jnp.take_along_axis(
        words, 4 * tile + lane // 32, axis=1, mode="promise_in_bounds"
    )
    bit = lax.shift_right_logical(spread, lane % 32) & 1
    return jnp.where(bit == 1, weight.astype(F32), 0.0).astype(BF)


def mask_gu_kernel(gate, gmask, up, umask, out, gw, uw):
    gw[:, 0:56] = gmask[...]
    uw[:, 0:56] = umask[...]

    def body(r, carry):
        rows = pl.ds(pl.multiple_of(r * 32, 32), 32)
        g, u = gw[rows, :], uw[rows, :]
        for j in range(14):
            cols = slice(j * 128, (j + 1) * 128)
            out[j, rows, 0:128] = kept(g, gate[rows, cols], j)
            out[j, rows, 128:256] = kept(u, up[rows, cols], j)
        return carry

    lax.fori_loop(0, gate.shape[0] // 32, body, 0)


def mask_gu(gate, gmask, up, umask):
    rows = 256
    wide = pl.BlockSpec((rows, 1792), lambda b: (b, 0))
    thin = pl.BlockSpec((rows, 56), lambda b: (b, 0))
    return pl.pallas_call(
        mask_gu_kernel,
        grid=(1024 // rows,),
        in_specs=[wide, thin, wide, thin],
        out_specs=pl.BlockSpec((14, rows, 256), lambda b: (0, b, 0)),
        out_shape=jax.ShapeDtypeStruct((14, 1024, 256), BF),
        scratch_shapes=[pltpu.VMEM((rows, 128), jnp.int32)] * 2,
    )(gate, gmask, up, umask)


def mask_down_kernel(weight, mask, out, words):
    words[:, 0:32] = mask[...]

    def body(r, carry):
        rows = pl.ds(pl.multiple_of(r * 32, 32), 32)
        w = words[rows, :]
        for j in range(8):
            cols = slice(j * 128, (j + 1) * 128)
            out[rows, cols] = kept(w, weight[rows, cols], j)
        return carry

    lax.fori_loop(0, weight.shape[0] // 32, body, 0)


def mask_down(weight, mask):
    rows = 256
    return pl.pallas_call(
        mask_down_kernel,
        grid=(1792 // rows,),
        in_specs=[
            pl.BlockSpec((rows, 1024), lambda b: (b, 0)),
            pl.BlockSpec((rows, 32), lambda b: (b, 0)),
        ],
        out_specs=pl.BlockSpec((rows, 1024), lambda b: (b, 0)),
        out_shape=jax.ShapeDtypeStruct((1792, 1024), BF),
        scratch_shapes=[pltpu.VMEM((rows, 128), jnp.int32)],
    )(weight, mask)


def main_kernel(
    nrm, gu_h, dn_h,
    out, inorm, hnorm,
    gu, dn, tok, rs, hid, p, psend, drecv, isq, isq_r, hsq, hsq_r,
    w_loc, w_send, w_recv, dn_loc, dn_send, dn_recv, a_loc,
    ax_send, ax_recv, af_send, af_recv, rs_send, rs_recv, ag_send, ag_recv,
    d_send, d_recv, n_send, n_recv,
):
    dp, mp = lax.axis_index("dp"), lax.axis_index("mp")
    x, c = dp // 2, dp % 2
    z, y = mp // 4, mp % 4
    sends = []

    def xs(k):
        return lax.rem(x + k + 4, 4)

    def at(xx, cc, zz, yy):
        return (xx * 2 + cc, zz * 4 + yy)

    peer = at(x, 1 - c, z, y)

    def remote(src, dst, ssem, rsem, dev):
        return pltpu.make_async_remote_copy(
            src_ref=src, dst_ref=dst, send_sem=ssem, recv_sem=rsem,
            device_id=dev, device_id_type=MESH,
        )

    def go(copy):
        copy.start()
        sends.append(copy)
        return copy

    mine = pl.ds(pl.multiple_of(c * 1024, 1024), 1024)

    def w_local(t):
        return pltpu.make_async_copy(gu_h.at[t], gu.at[t, mine], w_loc.at[t])

    def w_remote(t):
        return remote(gu_h.at[t], gu.at[t, mine], w_send.at[t], w_recv.at[t], peer)

    own = pltpu.make_async_copy(nrm.at[x], tok.at[x], a_loc.at[0])
    own.start()

    def load(n, carry):
        w_local(n).start()
        w_local(NT + n).start()
        return carry

    lax.fori_loop(0, NT, load, 0)
    dn_local = pltpu.make_async_copy(dn_h, dn.at[c], dn_loc.at[0])
    dn_local.start()

    barrier = pltpu.get_barrier_semaphore()
    for k in (1, 2, 3):
        pl.semaphore_signal(barrier, inc=1, device_id=at(xs(k), c, z, y), device_id_type=MESH)

    def greet(k, carry):
        other = lax.rem(c * 16 + mp + k, 32)
        pl.semaphore_signal(
            barrier, inc=1, device_id=(x * 2 + other // 16, other % 16), device_id_type=MESH
        )
        return carry

    lax.fori_loop(1, 32, greet, 0)
    pl.semaphore_wait(barrier, 34)

    def coord(g):
        return y if g % 2 == 0 else z

    def piece(g, w):
        return pl.ds(pl.multiple_of(g * R + w * 16, 16), 16)

    def ax(g, dx):
        rows = piece(g, coord(g))
        return remote(
            nrm.at[xs(dx), rows], tok.at[x, rows],
            ax_send.at[g, dx - 1], ax_recv.at[g, dx - 1], at(xs(dx), c, z, y),
        )

    def af(g, dx, dw):
        src = xs(-dx)
        rows = piece(g, coord(g))
        w = lax.rem(coord(g) + dw, 4)
        dev = at(x, c, z, w) if g % 2 == 0 else at(x, c, w, y)
        return remote(
            tok.at[src, rows], tok.at[src, rows],
            af_send.at[g, dx - 1, dw - 1], af_recv.at[g, dx - 1, dw - 1], dev,
        )

    for dx in (1, 3, 2):
        go(ax(0, dx))

    def send_w(n, carry):
        w_remote(n).start()
        w_remote(NT + n).start()
        return carry

    lax.fori_loop(0, NT, send_w, 0)
    for g in range(1, G):
        for dx in (1, 3, 2):
            go(ax(g, dx))
    dn_remote = remote(dn_h, dn.at[c], dn_send.at[0], dn_recv.at[0], peer)
    go(dn_remote)

    def forward_tokens(g):
        for dx in (1, 3, 2):
            ax(g, dx).wait_recv()
            for dw in (1, 3, 2):
                go(af(g, dx, dw))

    def wait_tokens(g, dx):
        for dw in (1, 2, 3):
            af(g, dx, dw).wait_recv()

    isq[...] = jnp.zeros_like(isq)
    hsq[...] = jnp.zeros_like(hsq)

    def rs_copy(s, d, g, h):
        return remote(
            rs.at[s, d, g, h], rs.at[s + 1, d, g, h],
            rs_send.at[s, d, g, h], rs_recv.at[s, d, g, h],
            at(xs(1 if d == 0 else -1), c, z, y),
        )

    def ag_copy(d, g, h, hop, block):
        return remote(
            hid.at[d, g, block, h], hid.at[d, g, block, h],
            ag_send.at[d, g, h, hop], ag_recv.at[d, g, h, hop],
            at(xs(1 if d == 0 else -1), c, z, y),
        )

    def rs_stage(g, s):
        rows = slice(g * R, (g + 1) * R)
        blocks = (xs(-s), xs(s))
        if s == 1:
            wait_tokens(g, 1)
            wait_tokens(g, 3)
        if s == 2:
            wait_tokens(g, 2)

        def tile(n, carry):
            if g == 0 and s == 0:
                for t in (n, NT + n):
                    w_local(t).wait()
                    w_remote(t).wait_recv()
            for d in (0, 1):
                p[d, n] = jnp.dot(
                    tok[blocks[d], rows], gu[d * NT + n], preferred_element_type=F32
                )
            return carry

        lax.fori_loop(0, NT, tile, 0)
        for h in (0, 1):
            part = slice(h * H, (h + 1) * H)
            for d in (0, 1):
                if s == 0:
                    rs[0, d, g, h] = p[d, :, part].astype(BF)
                elif s < 3:
                    rs_copy(s - 1, d, g, h).wait_recv()
                    rs[s, d, g, h] = (rs[s, d, g, h].astype(F32) + p[d, :, part]).astype(BF)
                else:
                    rs_copy(2, d, g, h).wait_recv()
                    for n in range(NT):
                        v = rs[3, d, g, h, n].astype(F32) + p[d, n, part]
                        gate, up = v[:, :128], v[:, 128:]
                        hidden = (gate / (1.0 + jnp.exp(-gate)) * up).astype(BF)
                        hid[d, g, blocks[d], h, :, n * 128 : (n + 1) * 128] = hidden
                    go(ag_copy(d, g, h, 0, blocks[d]))
                if s < 3:
                    go(rs_copy(s, d, g, h))

    def ag_block(d, hop):
        return xs(-hop) if d == 0 else xs(hop)

    def ag_wait(g, hop, onward):
        for h in (0, 1):
            for d in (0, 1):
                block = ag_block(d, hop)
                ag_copy(d, g, h, hop, block).wait_recv()
                if onward:
                    go(ag_copy(d, g, h, hop + 1, block))

    def token_squares(g):
        def body(t, carry):
            v = tok[t, g * R : (g + 1) * R].astype(F32)
            v = (v * v).reshape(R // 8, 8, FC).sum(axis=0)
            isq[0] += v[:, :1024]
            isq[1] += v[:, 1024:]
            return carry

        lax.fori_loop(0, NX, body, 0)

    def hidden_squares(g):
        def body(k, carry):
            for d in (0, 1):
                v = hid[d, g, k // 2, k % 2].astype(F32)
                hsq[d] += (v * v).reshape(H // 8, 8, UH).sum(axis=0)
            return carry

        lax.fori_loop(0, 2 * NX, body, 0)

    def own_piece(h):
        return y == 2 * c + h

    def d_copy(g, k, h, other):
        core = 1 - c if other else c
        block = lax.rem(z + k, 4)
        return remote(
            psend.at[g, core, block, h], drecv.at[g, mp],
            d_send.at[g, k, h, other], d_recv.at[g, mp],
            at(x, core, block, 2 * c + h),
        )

    def down(g):
        def tile(q, carry):
            core, col = q // 4, q % 4
            cols = pl.ds(pl.multiple_of(col * 256, 256), 256)
            acc = jnp.dot(
                hid[0, g].reshape(NX * R, UH), dn[core, 0:UH, cols], preferred_element_type=F32
            ) + jnp.dot(
                hid[1, g].reshape(NX * R, UH), dn[core, UH:, cols], preferred_element_type=F32
            )
            psend[g, core, :, :, :, cols] = acc.astype(BF).reshape(NX, 2, H, 256)
            return carry

        lax.fori_loop(0, 8, tile, 0)
        for k in (2, 1, 3, 0):
            for h in (0, 1):
                for other in (1, 0):
                    if k == 0 and other == 0:

                        @pl.when(own_piece(h))
                        def _():
                            drecv[g, mp] = psend[g, c, z, h]

                        @pl.when(jnp.logical_not(own_piece(h)))
                        def _():
                            d_copy(g, k, h, other).start()
                    else:
                        go(d_copy(g, k, h, other))

    def finish(g):
        mine_too = y // 2 == c

        def arrive(src, carry):
            @pl.when(jnp.logical_not(jnp.logical_and(mine_too, src == mp)))
            def _():
                remote(
                    psend.at[g, 0, 0, 0], drecv.at[g, src],
                    d_send.at[g, 0, 0, 0], d_recv.at[g, src], peer,
                ).wait_recv()

            return carry

        lax.fori_loop(0, 16, arrive, 0)
        for q in range(8):
            cols = slice(q * 128, (q + 1) * 128)
            total = drecv[g, 0, :, cols].astype(F32)
            for src in range(1, 16):
                total += drecv[g, src, :, cols].astype(F32)
            out[g * H : (g + 1) * H, cols] = total.astype(BF)

    forward_tokens(0)
    own.wait()
    rs_stage(0, 0)
    forward_tokens(1)
    rs_stage(0, 1)
    forward_tokens(2)
    rs_stage(0, 2)
    forward_tokens(3)
    rs_stage(0, 3)
    token_squares(0)
    for g in range(1, G):
        rs_stage(g, 0)
        ag_wait(g - 1, 0, True)
        rs_stage(g, 1)
        ag_wait(g - 1, 1, True)
        rs_stage(g, 2)
        token_squares(g)
        ag_wait(g - 1, 2, False)
        if g == 1:
            dn_local.wait()
            dn_remote.wait_recv()
        down(g - 1)
        rs_stage(g, 3)
        hidden_squares(g - 1)
        if g >= 2:
            finish(g - 2)
    i_copy = remote(isq.at[1 - c], isq_r, n_send.at[0], n_recv.at[0], peer)
    go(i_copy)
    ag_wait(G - 1, 0, True)
    ag_wait(G - 1, 1, True)
    i_copy.wait_recv()
    inorm[...] = jnp.sqrt(jnp.sum(isq[c] + isq_r[...], axis=0, keepdims=True))
    ag_wait(G - 1, 2, False)
    down(G - 1)
    hidden_squares(G - 1)
    h_copy = remote(hsq, hsq_r, n_send.at[1], n_recv.at[1], peer)
    go(h_copy)
    finish(G - 2)
    h_copy.wait_recv()
    for d in (0, 1):
        hnorm[:, d * UH : (d + 1) * UH] = jnp.sqrt(
            jnp.sum(hsq[d] + hsq_r[d], axis=0, keepdims=True)
        )
    finish(G - 1)

    def sent_w(n, carry):
        w_remote(n).wait_send()
        return carry

    lax.fori_loop(0, 2 * NT, sent_w, 0)
    for g in range(G):
        for h in (0, 1):

            @pl.when(jnp.logical_not(own_piece(h)))
            def _():
                d_copy(g, 0, h, 0).wait_send()

    for copy in sends:
        copy.wait_send()


def main_call(nrm, gu, dn):
    dma = pltpu.SemaphoreType.DMA
    vm = pltpu.VMEM
    anywhere = pl.BlockSpec(memory_space=pl.ANY)
    in_vmem = pl.BlockSpec(memory_space=pltpu.VMEM)
    return pl.pallas_call(
        main_kernel,
        in_specs=[anywhere] * 3,
        out_specs=[in_vmem] * 3,
        out_shape=[
            jax.ShapeDtypeStruct((128, 1024), BF),
            jax.ShapeDtypeStruct((1, 1024), F32),
            jax.ShapeDtypeStruct((1, 1792), F32),
        ],
        scratch_shapes=[
            vm((2 * NT, FC, 256), BF),
            vm((2, 1792, 1024), BF),
            vm((NX, RT, FC), BF),
            vm((4, 2, G, 2, NT, H, 256), BF),
            vm((2, G, NX, 2, H, UH), BF),
            vm((2, NT, R, 256), F32),
            vm((G, 2, NX, 2, H, 1024), BF),
            vm((G, 16, H, 1024), BF),
            vm((2, 8, 1024), F32),
            vm((8, 1024), F32),
            vm((2, 8, UH), F32),
            vm((2, 8, UH), F32),
            dma((2 * NT,)), dma((2 * NT,)), dma((2 * NT,)),
            dma((1,)), dma((1,)), dma((1,)), dma((1,)),
            dma((G, 3)), dma((G, 3)), dma((G, 3, 3)), dma((G, 3, 3)),
            dma((3, 2, G, 2)), dma((3, 2, G, 2)),
            dma((2, G, 2, 3)), dma((2, G, 2, 3)),
            dma((G, 4, 2, 2)), dma((G, 16)),
            dma((2,)), dma((2,)),
        ],
        compiler_params=pltpu.CompilerParams(
            collective_id=0, has_side_effects=True, vmem_limit_bytes=67043328 - 2**20
        ),
    )(nrm, gu, dn)


def on_device(
    tokens, norm_gain, gate_weight, gate_mask, up_weight, up_mask, down_weight, down_mask
):
    gu = mask_gu(gate_weight, gate_mask, up_weight, up_mask)
    dn = mask_down(down_weight, down_mask)
    nrm = norm_call(tokens, norm_gain)
    mixed, inorm, hnorm = main_call(nrm, gu, dn)
    return mixed, inorm.reshape(1024), hnorm.reshape(1792)


def solution(mesh):
    return jax.shard_map(
        on_device,
        mesh=mesh,
        in_specs=(
            P("dp", None), P(), P("dp", "mp"), P("dp", "mp"),
            P("dp", "mp"), P("dp", "mp"), P("mp", "dp"), P("mp", "dp"),
        ),
        out_specs=(P("mp", "dp"), P("dp"), P("mp")),
        check_vma=False,
    )
```

time: 347 us -> 198 us (0.57)
  waiting for transfers between devices: 217 us -> 0 us
  Pallas kernels: 0 us -> 187 us
  other arithmetic: 40.8 us -> 1.31 us
  matrix products: 32.5 us -> 0 us
  local copies, waits for them, and re-layouts: 32.7 us -> 8.05 us
  between operations: 13.9 us -> 0.64 us
  starting transfers between devices: 9.37 us -> 0 us
    pallas_call x0 -> x4, Pallas kernels: none -> 187 us  [the longest x1 159 us: main_call(): pl.pallas_call(main_kernel, in_specs=[anywhere] * 3, out_specs=[in_vmem]...]
    reduce_scatter x3 -> x0, waiting for transfers between devices: 146 us -> none  [the longest x1 83.1 us: on_device(): lax.psum_scatter(jnp.concatenate([gate_part, up_part], axis=1).astype(jnp...]
    all_gather x1 -> x0, waiting for transfers between devices: 37.9 us -> none  [on_device(): lax.all_gather(hidden, 'dp', axis=0, tiled=True)]
    all_to_all x2 -> x0, waiting for transfers between devices: 32.5 us -> none  [the longest x1 30.6 us: on_device(): lax.all_to_all(normed, 'dp', split_axis=1, concat_axis=0, tiled=True)]
    dot_general x3 -> x0, matrix products: 32.5 us -> none  [the longest x1 13.2 us: on_device(): jnp.dot(lax.all_gather(hidden, 'dp', axis=0, tiled=True), down_kept, pref...]
    concatenate x1 -> x0, other arithmetic: 17.1 us -> none  [on_device(): jnp.concatenate([gate_part, up_part], axis=1).astype(jnp.bfloat16)]
    unnamed x18 -> x7, local copies, waits for them, and re-layouts: 24.2 us -> 8.05 us
    select_n x2 -> x0, other arithmetic: 11.2 us -> none  [keep_entries(): return jnp.where(kept_bits == 1, weight, jnp.zeros_like(weight))]
  transfers between devices with their start and end apart: 6 -> 0, of which waited for: 6 -> 0; matrix products, arithmetic and copies ran while one was open for 10% -> 0% of each run, Pallas kernels for 0% -> 0%
where the time goes in v1:
time: 198 us; the launch traced here: 197 us
  Pallas kernels  187 us (94%)
  local copies, waits for them, and re-layouts  8.05 us (4%)
    pallas_call x1, Pallas kernels, main_call(): pl.pallas_call(main_kernel, in_specs=[anywhere] * 3, out_specs=[in_vmem]...  159 us
    pallas_call x1, Pallas kernels, mask_gu(): pl.pallas_call(mask_gu_kernel, grid=(1024 // rows,), in_specs=[wide, thin...  10.8 us
    pallas_call x1, Pallas kernels, mask_down(): pl.pallas_call(mask_down_kernel, grid=(1792 // rows,), in_specs=[pl.Block...  10 us
    unnamed x7, local copies, waits for them, and re-layouts  8.05 us
    pallas_call x1, Pallas kernels, norm_call(): pl.pallas_call(norm_kernel, grid=(2 * G,), in_specs=[pl.BlockSpec((H, 819...  7.6 us

profile of v1, /device:TPU:0, one launch (start us, length us, event | category | flops | bytes accessed | tf_op | source)
XLA Modules:
  0.0 197.1 jit_solution(816545563375164571)
XLA Ops:
  0.6 1.9 copy.11.gmask
  2.6 2.0 copy.12.umask
  4.5 0.0 copy-start
  4.5 10.8 %shard_map.104.gu_h = bf16[14,1024,256]{2,1,0:T(8,128)(2,1)} custom-call(bf16[1024,1792]{1,0:T(8,128)(2,1)} %gate.1, s32[1024,56]{1,0:T(8,128)} %copy.11.gmask, bf16[1024,1792]{1,0:T(8,128)(2,1)} %up.1, s32[1024,56]{1,0:T(8,128)} %copy.12.umask), custom_call_target="tpu_custom_call" | custom-call | tf_op jit(solution)/shard_map/pallas_call | solution.py:74
  15.3 0.0 copy-done
  15.3 1.2 copy.13.mask
  16.6 10.0 %shard_map.105.dn_h = bf16[1792,1024]{1,0:T(8,128)(2,1)} custom-call(bf16[1792,1024]{1,0:T(8,128)(2,1)} %weight.1, s32[1792,32]{1,0:T(8,128)} %copy.13.mask), custom_call_target="tpu_custom_call" | custom-call | tf_op jit(solution)/shard_map/pallas_call | solution.py:100
  26.6 7.6 %shard_map.103.nrm = bf16[4,256,2048]{2,1,0:T(8,128)(2,1)} custom-call(bf16[256,8192]{1,0:T(8,128)(2,1)} %tok_ref.1, f32[1,8192]{1,0:T(1,128)} %bitcast.2), custom_call_target="tpu_custom_call" | custom-call | tf_op jit(solution)/shard_map/pallas_call | solution.py:33
  34.2 158.7 %shard_map.106 = (bf16[128,1024]{1,0:T(8,128)(2,1)}, f32[1,1024]{1,0:T(1,128)}, f32[1,1792]{1,0:T(1,128)}) custom-call(bf16[4,256,2048]{2,1,0:T(8,128)(2,1)} %shard_map.103.nrm, bf16[14,1024,256]{2,1,0:T(8,128)(2,1)} %shard_map.104.gu_h, bf16[1792,1024]{1,0:T(8,128)(2,1)} %shard_map.105.dn_h), custom_call_target="tpu_custom_call" | custom-call | tf_op jit(solution)/shard_map/pallas_call | solution.py:441
  192.9 1.3 reduce
  194.2 1.7 copy.16
  195.8 1.3 copy.17
Async XLA Ops:
  4.5 10.8 %copy-start = (s32[1792,32]{0,1:T(8,128)S(1)}, s32[1792,32]{0,1:T(8,128)}, u32[]{:S(2)}) copy-start(s32[1792,32]{0,1:T(8,128)} %param.15) | copy-start | bytes 688132

commit v2 on v0

v2 whole, which is shorter than its diff:
```python
import jax
import jax.numpy as jnp
from jax import lax
from jax.experimental import pallas as pl
from jax.experimental.pallas import tpu as pltpu
from jax.sharding import PartitionSpec as P

MESH = pl.DeviceIdType.MESH
BF = jnp.bfloat16
F32 = jnp.float32

NX = 4
G = 4
U = 8
RT = 256
NT = 7
FC = 2048
UH = 896


def schedule():
    first, second = range(4), range(4, 8)
    plan = []
    for s in range(4):
        plan += [("product", 0, s)] + [("ring", u, s) for u in first]
        if s == 0:
            plan += [("norm", 2), ("norm", 3)]
        if s == 1:
            plan += [("pass", 2), ("pass", 3), ("down_mask", 0)]
        if s == 2:
            plan += [("down_mask", 1)]
    plan += [("squares", 0), ("product", 1, 0)] + [("ring", u, 0) for u in second]
    plan += [("hop", u, 1) for u in first]
    plan += [("product", 1, 1)] + [("ring", u, 1) for u in second]
    plan += [("hop", u, 2) for u in first]
    plan += [("product", 1, 2)] + [("ring", u, 2) for u in second]
    plan += [("down", 0, 2), ("down", 2, 2), ("product", 1, 3)]
    plan += [("ring", u, 3) for u in second]
    plan += [("squares", 1), ("token_norms",)]
    plan += [("hop", u, 1) for u in second]
    plan += [("finish", u) for u in first[:2]]
    plan += [("hop", u, 2) for u in second]
    plan += [("finish", u) for u in first[2:]]
    plan += [("down", u, 1) for u in second]
    plan += [("hidden_norms",)]
    plan += [("finish", u) for u in second]
    return plan


def main_kernel(
    tok_h, gain, gate_h, gmask_h, up_h, umask_h, dn_h, dmask_h,
    out, inorm, hnorm,
    gu, dn, tok, rs, hid, p, psend, drecv, tk, scl, nsend, wt, lhs, e,
    isq, isq_r, hsq, hsq_r,
    t_sem, m_sem, w_loc, w_send, w_recv, dn_loc, dn_send, dn_recv,
    ax_send, ax_recv, af_send, af_recv, rs_send, rs_recv, ag_send, ag_recv,
    d_send, d_recv, n_send, n_recv,
):
    dp, mp = lax.axis_index("dp"), lax.axis_index("mp")
    x, c = dp // 2, dp % 2
    z, y = mp // 4, mp % 4
    sends = []

    def xs(k):
        return lax.rem(x + k + 4, 4)

    def at(xx, cc, zz, yy):
        return (xx * 2 + cc, zz * 4 + yy)

    peer = at(x, 1 - c, z, y)

    def remote(src, dst, ssem, rsem, dev):
        return pltpu.make_async_remote_copy(
            src_ref=src, dst_ref=dst, send_sem=ssem, recv_sem=rsem,
            device_id=dev, device_id_type=MESH,
        )

    def go(copy):
        copy.start()
        sends.append(copy)

    mine = pl.ds(pl.multiple_of(c * 1024, 1024), 1024)

    def t_local(g, h):
        rows = slice(h * 128 + g * 32, h * 128 + g * 32 + 32)
        return pltpu.make_async_copy(tok_h.at[rows], tk.at[g, h], t_sem.at[g, h])

    def w_local(t, q):
        src = (gate_h, up_h)[q].at[:, pl.ds(pl.multiple_of(t * 128, 128), 128)]
        dst = gu.at[t, mine, pl.ds(q * 128, 128)]
        return pltpu.make_async_copy(src, dst, w_loc.at[t, q])

    def w_remote(t):
        tile = gu.at[t, mine]
        return remote(tile, tile, w_send.at[t], w_recv.at[t], peer)

    g_words = pltpu.make_async_copy(gmask_h, wt.at[0:56, 0:1024], m_sem.at[0])
    u_words = pltpu.make_async_copy(umask_h, wt.at[64:120, 0:1024], m_sem.at[1])
    d_words = pltpu.make_async_copy(dmask_h, wt.at[0:32], m_sem.at[2])
    dn_local = pltpu.make_async_copy(dn_h, dn.at[c], dn_loc.at[0])

    def dn_remote(k):
        rows = slice(k * 896, (k + 1) * 896)
        return remote(dn.at[c, rows], dn.at[c, rows], dn_send.at[k], dn_recv.at[k], peer)

    for g in range(2):
        for h in (0, 1):
            t_local(g, h).start()
    g_words.start()
    u_words.start()

    def load(t, carry):
        w_local(t, 0).start()
        w_local(t, 1).start()
        return carry

    lax.fori_loop(0, 2 * NT, load, 0)
    for g in range(2, 4):
        for h in (0, 1):
            t_local(g, h).start()
    dn_local.start()

    barrier = pltpu.get_barrier_semaphore()
    for k in (1, 2, 3):
        pl.semaphore_signal(barrier, inc=1, device_id=at(xs(k), c, z, y), device_id_type=MESH)

    def greet(k, carry):
        other = lax.rem(c * 16 + mp + k, 32)
        pl.semaphore_signal(
            barrier, inc=1, device_id=(x * 2 + other // 16, other % 16), device_id_type=MESH
        )
        return carry

    lax.fori_loop(1, 32, greet, 0)

    k = lax.broadcasted_iota(jnp.int32, (256, 1792), 0)
    col = lax.broadcasted_iota(jnp.int32, (256, 1792), 1)
    e[...] = jnp.where((k % 64 == col // 32) & (k // 64 == (col % 32) // 8), 1.0, 0.0).astype(BF)
    wt[56:64] = jnp.zeros((8, 1792), jnp.int32)
    wt[120:128] = jnp.zeros((8, 1792), jnp.int32)
    wt[32:56, 1024:] = jnp.zeros((24, 768), jnp.int32)
    wt[64:120, 1024:] = jnp.zeros((56, 768), jnp.int32)
    isq[...] = jnp.zeros_like(isq)
    hsq[...] = jnp.zeros_like(hsq)

    def coord(g):
        return y if g % 2 == 0 else z

    def piece(g, w):
        return pl.ds(pl.multiple_of(g * 64 + w * 16, 16), 16)

    def block_cols(b):
        return pl.ds(pl.multiple_of(b * FC, FC), FC)

    def ax(g, dx):
        return remote(
            nsend.at[g, dx - 1], tok.at[x, piece(g, coord(g))],
            ax_send.at[g, dx - 1], ax_recv.at[g, dx - 1], at(xs(dx), c, z, y),
        )

    def af(g, dx, dw):
        src = xs(-dx)
        rows = piece(g, coord(g))
        w = lax.rem(coord(g) + dw, 4)
        dev = at(x, c, z, w) if g % 2 == 0 else at(x, c, w, y)
        return remote(
            tok.at[src, rows], tok.at[src, rows],
            af_send.at[g, dx - 1, dw - 1], af_recv.at[g, dx - 1, dw - 1], dev,
        )

    def normed(g, h, rows, b):
        cols = block_cols(b)
        v = tk[g, h, rows, cols].astype(F32)
        return (v * scl[g, h, rows, 0:1] * gain[:, cols]).astype(BF)

    def norm(g):
        for h in (0, 1):
            t_local(g, h).wait()
        for h in (0, 1):
            for i in (0, 16):
                rows = slice(i, i + 16)
                total = jnp.zeros((16, 512), F32)
                for b in range(16):
                    v = tk[g, h, rows, b * 512 : (b + 1) * 512].astype(F32)
                    total += v * v
                total = jnp.sum(total, axis=1, keepdims=True)
                scale = lax.rsqrt(total * (1.0 / 8192) + 1e-05)
                scl[g, h, rows] = jnp.broadcast_to(scale, (16, 128))
        w = coord(g)
        rows = pl.ds(pl.multiple_of((w // 2) * 16, 16), 16)
        for dx in (1, 3, 2):
            nsend[g, dx - 1] = normed(g, w % 2, rows, xs(dx))
        if g == 0:
            pl.semaphore_wait(barrier, 34)
        for dx in (1, 3, 2):
            go(ax(g, dx))
        for h in (0, 1):
            for i in (0, 1):
                start = g * 64 + i * 32 + h * 16
                tok[x, start : start + 16] = normed(g, h, slice(i * 16, i * 16 + 16), x)

    def pass_on(g):
        for dx in (1, 3, 2):
            ax(g, dx).wait_recv()
            for dw in (1, 3, 2):
                go(af(g, dx, dw))

    def spread_words(at_row, count, both):
        low = lax.broadcasted_iota(jnp.int32, (128, 128), 1) < 64

        def body(r, carry):
            start = pl.multiple_of(r * 128, 128)
            rows = pl.ds(start, 128)
            w = jnp.transpose(wt[:, rows])
            b = [(lax.shift_right_logical(w, 8 * i) & 255).astype(F32) for i in range(4)]
            t = [pltpu.roll(v, 64, 1) for v in b]
            lhs[rows, 0:128] = jnp.where(low, b[0], t[1]).astype(BF)
            lhs[rows, 128:256] = jnp.where(low, b[2], t[3]).astype(BF)
            if both:
                upper = pl.ds(start + 1024, 128)
                lhs[upper, 0:128] = jnp.where(low, t[0], b[1]).astype(BF)
                lhs[upper, 128:256] = jnp.where(low, t[2], b[3]).astype(BF)
            return carry

        lax.fori_loop(at_row, at_row + count, body, 0)

    bit_of = lax.shift_left(1, lax.broadcasted_iota(jnp.int32, (256, 256), 1) % 8)

    def bits(row, pair):
        cols = pl.ds(pl.multiple_of(pair * 256, 256), 256)
        byte = jnp.dot(lhs[pl.ds(row, 256)], e[:, cols], preferred_element_type=F32)
        return (byte.astype(jnp.int32) & bit_of) != 0

    def mask_pair(j, carry):
        for q in (0, 1):
            for i in (0, 1):
                w_local(2 * j + i, q).wait()

        def body(r, carry):
            start = pl.multiple_of(r * 256, 256)
            rows = pl.ds(pl.multiple_of(c * 1024 + start, 256), 256)
            for q in (0, 1):
                keep = bits(pl.multiple_of(q * 1024 + start, 256), j)
                cols = slice(q * 128, (q + 1) * 128)
                for i in (0, 1):
                    v = gu[2 * j + i, rows, cols].astype(F32)
                    v = jnp.where(keep[:, i * 128 : (i + 1) * 128], v, 0.0)
                    gu[2 * j + i, rows, cols] = v.astype(BF)
            return carry

        lax.fori_loop(0, 4, body, 0)
        w_remote(2 * j).start()
        w_remote(2 * j + 1).start()
        return carry

    def down_mask(k):
        if k == 0:
            d_words.wait()
            spread_words(0, 14, False)
            dn_local.wait()

        def body(r, carry):
            start = pl.multiple_of(k * 896 + r * 128, 128)
            rows = pl.ds(start, 128)
            for j in range(4):
                cols = slice(j * 256, (j + 1) * 256)
                byte = jnp.dot(lhs[rows], e[:, cols], preferred_element_type=F32)
                keep = (byte.astype(jnp.int32) & bit_of[:128]) != 0
                v = dn[c, rows, cols].astype(F32)
                dn[c, rows, cols] = jnp.where(keep, v, 0.0).astype(BF)
            return carry

        lax.fori_loop(0, 7, body, 0)
        go(dn_remote(k))

    def rs_copy(s, d, u):
        return remote(
            rs.at[s, d, u], rs.at[s + 1, d, u], rs_send.at[s, d, u], rs_recv.at[s, d, u],
            at(xs(1 if d == 0 else -1), c, z, y),
        )

    def ag_copy(d, u, hop, block):
        return remote(
            hid.at[d, u, block], hid.at[d, u, block],
            ag_send.at[d, u, hop], ag_recv.at[d, u, hop],
            at(xs(1 if d == 0 else -1), c, z, y),
        )

    def product(q, s):
        rows = slice(q * 128, (q + 1) * 128)
        blocks = (xs(-s), xs(s))
        if s in (1, 2):
            for g in (2 * q, 2 * q + 1):
                for dx in ((1, 3), (2,))[s - 1]:
                    for dw in (1, 2, 3):
                        af(g, dx, dw).wait_recv()

        def tile(n, carry):
            if q == 0 and s == 0:
                w_remote(n).wait_recv()
                w_remote(NT + n).wait_recv()
            for d in (0, 1):
                p[s, d, n] = jnp.dot(
                    tok[blocks[d], rows], gu[d * NT + n], preferred_element_type=F32
                )
            return carry

        lax.fori_loop(0, NT, tile, 0)

    def ring(u, s):
        part = slice((u % 4) * 32, (u % 4) * 32 + 32)
        for d in (0, 1):
            if s:
                rs_copy(s - 1, d, u).wait_recv()
            if s == 0:
                rs[0, d, u] = p[0, d, :, part].astype(BF)
            elif s < 3:
                rs[s, d, u] = (rs[s, d, u].astype(F32) + p[s, d, :, part]).astype(BF)
            if s < 3:
                go(rs_copy(s, d, u))
                continue
            block = xs(1) if d == 0 else xs(-1)
            for n in range(NT):
                v = rs[3, d, u, n].astype(F32) + p[3, d, n, part]
                gate, up = v[:, :128], v[:, 128:]
                hidden = (gate / (1.0 + jnp.exp(-gate)) * up).astype(BF)
                hid[d, u, block, :, :, n * 128 : (n + 1) * 128] = hidden.reshape(2, 16, 128)
            go(ag_copy(d, u, 0, block))

    def arrived(u, hop):
        for d in (0, 1):
            block = xs(-hop) if d == 0 else xs(hop)
            ag_copy(d, u, hop, block).wait_recv()
            if hop < 2:
                go(ag_copy(d, u, hop + 1, block))

    def squares(q):
        def body(t, carry):
            rows = pl.ds(pl.multiple_of(q * 128 + (t % 4) * 32, 32), 32)
            v = tok[t // 4, rows].astype(F32)
            v = (v * v).reshape(4, 8, FC).sum(axis=0)
            isq[0] += v[:, :1024]
            isq[1] += v[:, 1024:]
            return carry

        lax.fori_loop(0, 16, body, 0)

    def hidden_squares(u):
        def body(t, carry):
            for d in (0, 1):
                v = hid[d, u, t].reshape(32, UH).astype(F32)
                hsq[d] += (v * v).reshape(4, 8, UH).sum(axis=0)
            return carry

        lax.fori_loop(0, NX, body, 0)

    def d_copy(u, i):
        k, h, other = i // 4, (i // 2) % 2, i % 2
        core = lax.rem(c + other, 2)
        block = lax.rem(z + k, 4)
        return remote(
            psend.at[u, core, block, h], drecv.at[u, mp], d_send.at[u, i], d_recv.at[u, mp],
            at(x, core, block, 2 * c + h),
        )

    def kept_here(i):
        return jnp.logical_and(i // 4 == 0, jnp.logical_and(i % 2 == 0, y == 2 * c + (i // 2) % 2))

    def down(u, count):
        for v in range(u, u + count):
            arrived(v, 2)
        if u == 0:
            for k in (0, 1):
                dn_remote(k).wait_recv()

        def tile(t, carry):
            core, col = t // 4, t % 4
            cols = pl.ds(pl.multiple_of(col * 256, 256), 256)
            acc = sum(
                jnp.dot(
                    hid[d, u : u + count].reshape(count * 128, UH),
                    dn[core, d * UH : (d + 1) * UH, cols],
                    preferred_element_type=F32,
                )
                for d in (0, 1)
            )
            psend[u : u + count, core, :, :, :, cols] = acc.astype(BF).reshape(
                count, NX, 2, 16, 256
            )
            return carry

        lax.fori_loop(0, 8, tile, 0)

        def send(i, carry):
            i = lax.rem(i + 4, 16)
            for v in range(u, u + count):

                @pl.when(jnp.logical_not(kept_here(i)))
                def _():
                    d_copy(v, i).start()

            return carry

        lax.fori_loop(0, 16, send, 0)

        @pl.when(y // 2 == c)
        def _():
            for v in range(u, u + count):
                drecv[v, mp] = psend[v, c, z, y % 2]

        for v in range(u, u + count):
            hidden_squares(v)

    def finish(u):
        def arrive(src, carry):
            @pl.when(jnp.logical_not(jnp.logical_and(y // 2 == c, src == mp)))
            def _():
                remote(
                    psend.at[u, 0, 0, 0], drecv.at[u, src], d_send.at[u, 0], d_recv.at[u, src], peer
                ).wait_recv()

            return carry

        lax.fori_loop(0, 16, arrive, 0)
        for t in range(2):
            cols = slice(t * 512, (t + 1) * 512)
            total = drecv[u, 0, :, cols].astype(F32)
            for src in range(1, 16):
                total += drecv[u, src, :, cols].astype(F32)
            out[u * 16 : (u + 1) * 16, cols] = total.astype(BF)

    def token_norms():
        copy = remote(isq.at[1 - c], isq_r, n_send.at[0], n_recv.at[0], peer)
        go(copy)
        copy.wait_recv()
        inorm[...] = jnp.sqrt(jnp.sum(isq[c] + isq_r[...], axis=0, keepdims=True))

    def hidden_norms():
        copy = remote(hsq, hsq_r, n_send.at[1], n_recv.at[1], peer)
        go(copy)
        copy.wait_recv()
        for d in (0, 1):
            hnorm[:, d * UH : (d + 1) * UH] = jnp.sqrt(
                jnp.sum(hsq[d] + hsq_r[d], axis=0, keepdims=True)
            )

    tasks = dict(
        norm=norm, product=product, ring=ring, hop=lambda u, h: arrived(u, h - 1), down=down,
        finish=finish, squares=squares, token_norms=token_norms, hidden_norms=hidden_norms,
        down_mask=down_mask,
    )
    tasks["pass"] = pass_on

    with jax.named_scope("norm"):
        norm(0)
        norm(1)
    with jax.named_scope("words"):
        g_words.wait()
        u_words.wait()
        spread_words(0, 8, True)
        d_words.start()
    with jax.named_scope("mask"):
        lax.fori_loop(0, 4, mask_pair, 0)
    with jax.named_scope("pass"):
        pass_on(0)
        pass_on(1)
    with jax.named_scope("mask"):
        lax.fori_loop(4, NT, mask_pair, 0)
    for task in schedule():
        with jax.named_scope("_".join(str(v) for v in task)):
            tasks[task[0]](*task[1:])

    with jax.named_scope("sent"):

        def sent_w(n, carry):
            w_remote(n).wait_send()
            return carry

        lax.fori_loop(0, 2 * NT, sent_w, 0)

        def sent_d(i, carry):
            for u in range(U):

                @pl.when(jnp.logical_not(kept_here(i)))
                def _():
                    d_copy(u, i).wait_send()

            return carry

        lax.fori_loop(0, 16, sent_d, 0)
        for copy in sends:
            copy.wait_send()


def main_call(*args):
    dma = pltpu.SemaphoreType.DMA
    vm = pltpu.VMEM
    anywhere = pl.BlockSpec(memory_space=pl.ANY)
    in_vmem = pl.BlockSpec(memory_space=pltpu.VMEM)
    return pl.pallas_call(
        main_kernel,
        in_specs=[anywhere, in_vmem] + [anywhere] * 6,
        out_specs=[in_vmem] * 3,
        out_shape=[
            jax.ShapeDtypeStruct((128, 1024), BF),
            jax.ShapeDtypeStruct((1, 1024), F32),
            jax.ShapeDtypeStruct((1, 1792), F32),
        ],
        scratch_shapes=[
            vm((2 * NT, FC, 256), BF),
            vm((2, 1792, 1024), BF),
            vm((NX, RT, FC), BF),
            vm((4, 2, U, NT, 32, 256), BF),
            vm((2, U, NX, 2, 16, UH), BF),
            vm((4, 2, NT, 128, 256), F32),
            vm((U, 2, NX, 2, 16, 1024), BF),
            vm((U, 16, 16, 1024), BF),
            vm((G, 2, 32, 8192), BF),
            vm((G, 2, 32, 128), F32),
            vm((G, 3, 16, FC), BF),
            vm((128, 1792), jnp.int32),
            vm((2048, 256), BF),
            vm((256, 1792), BF),
            vm((2, 8, 1024), F32),
            vm((8, 1024), F32),
            vm((2, 8, UH), F32),
            vm((2, 8, UH), F32),
            dma((G, 2)), dma((3,)), dma((2 * NT, 2)), dma((2 * NT,)), dma((2 * NT,)),
            dma((1,)), dma((2,)), dma((2,)),
            dma((G, 3)), dma((G, 3)), dma((G, 3, 3)), dma((G, 3, 3)),
            dma((3, 2, U)), dma((3, 2, U)),
            dma((2, U, 3)), dma((2, U, 3)),
            dma((U, 16)), dma((U, 16)),
            dma((2,)), dma((2,)),
        ],
        compiler_params=pltpu.CompilerParams(
            collective_id=0, has_side_effects=True, vmem_limit_bytes=67043328
        ),
    )(*args)


def on_device(
    tokens, norm_gain, gate_weight, gate_mask, up_weight, up_mask, down_weight, down_mask
):
    mixed, inorm, hnorm = main_call(
        tokens, norm_gain.reshape(1, 8192), gate_weight, gate_mask.T, up_weight, up_mask.T,
        down_weight, down_mask.T,
    )
    return mixed, inorm.reshape(1024), hnorm.reshape(1792)


def solution(mesh):
    return jax.shard_map(
        on_device,
        mesh=mesh,
        in_specs=(
            P("dp", None), P(), P("dp", "mp"), P("dp", "mp"),
            P("dp", "mp"), P("dp", "mp"), P("mp", "dp"), P("mp", "dp"),
        ),
        out_specs=(P("mp", "dp"), P("dp"), P("mp")),
        check_vma=False,
    )
```

time: 347 us -> 167 us (0.48)
  waiting for transfers between devices: 217 us -> 0 us
  Pallas kernels: 0 us -> 160 us
  other arithmetic: 40.8 us -> 1.31 us
  matrix products: 32.5 us -> 0 us
  local copies, waits for them, and re-layouts: 32.7 us -> 2.94 us
  between operations: 13.9 us -> 0.64 us
  starting transfers between devices: 9.37 us -> 0 us
    pallas_call x0 -> x1, Pallas kernels: none -> 160 us  [main_call(): pl.pallas_call(main_kernel, in_specs=[anywhere, in_vmem] + [anywhere] * 6...]
    reduce_scatter x3 -> x0, waiting for transfers between devices: 146 us -> none  [the longest x1 83.1 us: on_device(): lax.psum_scatter(jnp.concatenate([gate_part, up_part], axis=1).astype(jnp...]
    all_gather x1 -> x0, waiting for transfers between devices: 37.9 us -> none  [on_device(): lax.all_gather(hidden, 'dp', axis=0, tiled=True)]
    all_to_all x2 -> x0, waiting for transfers between devices: 32.5 us -> none  [the longest x1 30.6 us: on_device(): lax.all_to_all(normed, 'dp', split_axis=1, concat_axis=0, tiled=True)]
    dot_general x3 -> x0, matrix products: 32.5 us -> none  [the longest x1 13.2 us: on_device(): jnp.dot(lax.all_gather(hidden, 'dp', axis=0, tiled=True), down_kept, pref...]
    unnamed x18 -> x2, local copies, waits for them, and re-layouts: 24.2 us -> 2.94 us
    concatenate x1 -> x0, other arithmetic: 17.1 us -> none  [on_device(): jnp.concatenate([gate_part, up_part], axis=1).astype(jnp.bfloat16)]
    select_n x2 -> x0, other arithmetic: 11.2 us -> none  [keep_entries(): return jnp.where(kept_bits == 1, weight, jnp.zeros_like(weight))]
  transfers between devices with their start and end apart: 6 -> 0, of which waited for: 6 -> 0; matrix products, arithmetic and copies ran while one was open for 10% -> 0% of each run, Pallas kernels for 0% -> 0%
where the time goes in v2:
time: 167 us; the launch traced here: 165 us
  Pallas kernels  160 us (96%)
  local copies, waits for them, and re-layouts  2.94 us (2%)
    pallas_call x1, Pallas kernels, main_call(): pl.pallas_call(main_kernel, in_specs=[anywhere, in_vmem] + [anywhere] * 6...  160 us

profile of v2, /device:TPU:0, one launch (start us, length us, event | category | flops | bytes accessed | tf_op | source)
XLA Modules:
  0.0 165.3 jit_solution(17293218487927246660)
XLA Ops:
  0.6 160.4 %shard_map.103 = (bf16[128,1024]{1,0:T(8,128)(2,1)}, f32[1,1024]{1,0:T(1,128)}, f32[1,1792]{1,0:T(1,128)}) custom-call(bf16[256,8192]{1,0:T(8,128)(2,1)} %tok_h.1, f32[1,8192]{1,0:T(1,128)} %bitcast.8, bf16[1024,1792]{1,0:T(8,128)(2,1)} %gate_h.1, s32[56,1024]{1,0:T(8,128)} %bitcast.5, bf16[1024,1792]{1,0:T(8,128)(2,1)} %up_h.1, s32[56,1024]{1,0:T(8,128)} %bitcast.6, ...), custom_call_target="tpu_custom_call" | custom-call | tf_op jit(solution)/shard_map/pallas_call | solution.py:500
  161.0 1.3 reduce
  162.4 1.7 %copy.13 = bf16[128,1024]{1,0:T(8,128)(2,1)} copy(bf16[128,1024]{1,0:T(8,128)(2,1)} %get-tuple-element.12) | data formatting | bytes 524288
  164.0 1.3 copy.14

commit v3 on v2

v3 whole, which is shorter than its diff:
```python
import jax
import jax.numpy as jnp
from jax import lax
from jax.experimental import pallas as pl
from jax.experimental.pallas import tpu as pltpu
from jax.sharding import PartitionSpec as P

MESH = pl.DeviceIdType.MESH
BF = jnp.bfloat16
F32 = jnp.float32

NX = 4
G = 4
U = 8
RT = 256
NT = 7
FC = 2048
UH = 896


SCHEDULE = (
    ("pass", 0), ("pass", 1), ("product", 0, 0), ("ring", 2, 0), ("ring", 0, 0), ("ring", 1, 0),
    ("ring", 3, 0), ("product", 1, 0), ("ring", 4, 0), ("down_mask", 0), ("pass", 3),
    ("pass", 2), ("product", 0, 1), ("ring", 0, 1), ("product", 0, 2), ("ring", 2, 1),
    ("ring", 1, 1), ("ring", 3, 1), ("ring", 0, 2), ("product", 0, 3), ("product", 1, 1),
    ("ring", 1, 2), ("ring", 0, 3), ("ring", 2, 2), ("ring", 3, 2), ("ring", 1, 3),
    ("hop", 0, 1), ("product", 1, 2), ("ring", 6, 0), ("ring", 4, 1), ("ring", 7, 0),
    ("down_mask", 1), ("ring", 3, 3), ("ring", 2, 3), ("squares", 0), ("ring", 4, 2),
    ("hop", 1, 1), ("product", 1, 3), ("hop", 2, 1), ("hop", 0, 2), ("ring", 4, 3),
    ("hop", 1, 2), ("ring", 6, 1), ("ring", 7, 1), ("ring", 5, 0), ("down", 0, 2), ("hop", 4, 1),
    ("hop", 3, 1), ("ring", 5, 1), ("hop", 4, 2), ("ring", 7, 2), ("hop", 2, 2), ("hop", 3, 2),
    ("ring", 5, 2), ("down", 4, 1), ("ring", 7, 3), ("ring", 6, 2), ("down", 2, 2),
    ("hop", 7, 1), ("ring", 5, 3), ("ring", 6, 3), ("hop", 7, 2), ("hop", 5, 1), ("hop", 6, 1),
    ("down", 7, 1), ("hop", 6, 2), ("finish", 0), ("hop", 5, 2), ("down", 6, 1), ("down", 5, 1),
    ("squares", 1), ("token_norms",), ("finish", 1), ("finish", 6), ("finish", 2), ("finish", 3),
    ("finish", 7), ("finish", 4), ("hidden_norms",), ("finish", 5),
)


def main_kernel(
    tok_h, gain, gate_h, gmask_h, up_h, umask_h, dn_h, dmask_h,
    out, inorm, hnorm,
    gu, dn, tok, rs, hid, p, psend, drecv, tk, scl, nsend, wt, lhs, e,
    isq, isq_r, hsq, hsq_r,
    t_sem, m_sem, w_loc, w_send, w_recv, dn_loc, dn_send, dn_recv,
    ax_send, ax_recv, af_send, af_recv, rs_send, rs_recv, ag_send, ag_recv,
    d_send, d_recv, n_send, n_recv,
):
    dp, mp = lax.axis_index("dp"), lax.axis_index("mp")
    x, c = dp // 2, dp % 2
    z, y = mp // 4, mp % 4
    def xs(k):
        return lax.rem(x + k + 4, 4)

    def at(xx, cc, zz, yy):
        return (xx * 2 + cc, zz * 4 + yy)

    peer = at(x, 1 - c, z, y)

    def remote(src, dst, ssem, rsem, dev):
        return pltpu.make_async_remote_copy(
            src_ref=src, dst_ref=dst, send_sem=ssem, recv_sem=rsem,
            device_id=dev, device_id_type=MESH,
        )

    def came(ref, sem):
        pltpu.make_async_copy(ref, ref, sem).wait()

    mine = pl.ds(pl.multiple_of(c * 1024, 1024), 1024)

    def t_local(g, h):
        rows = slice(h * 128 + g * 32, h * 128 + g * 32 + 32)
        return pltpu.make_async_copy(tok_h.at[rows], tk.at[g, h], t_sem.at[g])

    def w_local(t, q):
        src = (gate_h, up_h)[q].at[:, pl.ds(pl.multiple_of(t * 128, 128), 128)]
        dst = gu.at[t, mine, pl.ds(q * 128, 128)]
        return pltpu.make_async_copy(src, dst, w_loc.at[t // 2])

    def w_remote(t):
        tile = gu.at[t, mine]
        return remote(tile, tile, w_send.at[0], w_recv.at[lax.rem(t, NT)], peer)

    g_words = pltpu.make_async_copy(gmask_h, wt.at[0:56, 0:1024], m_sem.at[0])
    u_words = pltpu.make_async_copy(umask_h, wt.at[64:120, 0:1024], m_sem.at[1])
    d_words = pltpu.make_async_copy(dmask_h, wt.at[0:32], m_sem.at[2])
    dn_local = pltpu.make_async_copy(dn_h, dn.at[c], dn_loc.at[0])

    def dn_remote(k):
        rows = slice(k * 896, (k + 1) * 896)
        return remote(dn.at[c, rows], dn.at[c, rows], dn_send.at[0], dn_recv.at[0], peer)

    g_words.start()
    u_words.start()
    for g in (0, 1):
        for h in (0, 1):
            t_local(g, h).start()

    def load(t, carry):
        w_local(t, 0).start()
        w_local(t, 1).start()
        return carry

    lax.fori_loop(0, 2 * NT, load, 0)
    for g in (2, 3):
        for h in (0, 1):
            t_local(g, h).start()
    dn_local.start()

    barrier = pltpu.get_barrier_semaphore()
    for k in (1, 2, 3):
        pl.semaphore_signal(barrier, inc=1, device_id=at(xs(k), c, z, y), device_id_type=MESH)

    def greet(k, carry):
        other = lax.rem(c * 16 + mp + k, 32)
        pl.semaphore_signal(
            barrier, inc=1, device_id=(x * 2 + other // 16, other % 16), device_id_type=MESH
        )
        return carry

    lax.fori_loop(1, 32, greet, 0)

    k = lax.broadcasted_iota(jnp.int32, (256, 1792), 0)
    col = lax.broadcasted_iota(jnp.int32, (256, 1792), 1)
    e[...] = jnp.where((k % 64 == col // 32) & (k // 64 == (col % 32) // 8), 1.0, 0.0).astype(BF)
    wt[56:64] = jnp.zeros((8, 1792), jnp.int32)
    wt[120:128] = jnp.zeros((8, 1792), jnp.int32)
    wt[32:56, 1024:] = jnp.zeros((24, 768), jnp.int32)
    wt[64:120, 1024:] = jnp.zeros((56, 768), jnp.int32)
    isq[...] = jnp.zeros_like(isq)
    hsq[...] = jnp.zeros_like(hsq)

    def coord(g):
        return y if g % 2 == 0 else z

    def piece(g, w):
        return pl.ds(pl.multiple_of(g * 64 + w * 16, 16), 16)

    def block_cols(b):
        return pl.ds(pl.multiple_of(b * FC, FC), FC)

    def ax(g, dx):
        return remote(
            nsend.at[g, dx - 1], tok.at[x, piece(g, coord(g))],
            ax_send.at[0], ax_recv.at[g], at(xs(dx), c, z, y),
        )

    def af(g, dx, dw):
        src = xs(-dx)
        rows = piece(g, coord(g))
        w = lax.rem(coord(g) + dw, 4)
        dev = at(x, c, z, w) if g % 2 == 0 else at(x, c, w, y)
        return remote(
            tok.at[src, rows], tok.at[src, rows],
            af_send.at[0], af_recv.at[g // 2, dx % 2], dev,
        )

    def normed(g, h, rows, b):
        cols = block_cols(b)
        v = tk[g, h, rows, cols].astype(F32)
        return (v * scl[g, h, rows, 0:1] * gain[:, cols]).astype(BF)

    def norm(g):
        came(tk.at[g], t_sem.at[g])
        for h in (0, 1):
            for i in (0, 16):
                rows = slice(i, i + 16)
                total = jnp.zeros((16, 512), F32)
                for b in range(16):
                    v = tk[g, h, rows, b * 512 : (b + 1) * 512].astype(F32)
                    total += v * v
                total = jnp.sum(total, axis=1, keepdims=True)
                scale = lax.rsqrt(total * (1.0 / 8192) + 1e-05)
                scl[g, h, rows] = jnp.broadcast_to(scale, (16, 128))
        w = coord(g)
        rows = pl.ds(pl.multiple_of((w // 2) * 16, 16), 16)
        for dx in (1, 3, 2):
            nsend[g, dx - 1] = normed(g, w % 2, rows, xs(dx))
        for h in (0, 1):
            for i in (0, 1):
                start = g * 64 + i * 32 + h * 16
                tok[x, start : start + 16] = normed(g, h, slice(i * 16, i * 16 + 16), x)

    def send_tokens(g):
        for dx in (1, 3, 2):
            ax(g, dx).start()

    def pass_on(g):
        came(tok.at[0, 0:48], ax_recv.at[g])
        for dx in (1, 3, 2):
            for dw in (1, 3, 2):
                af(g, dx, dw).start()

    def spread_words(at_row, count, both):
        low = lax.broadcasted_iota(jnp.int32, (128, 128), 1) < 64

        def body(r, carry):
            start = pl.multiple_of(r * 128, 128)
            rows = pl.ds(start, 128)
            w = jnp.transpose(wt[:, rows])
            b = [(lax.shift_right_logical(w, 8 * i) & 255).astype(F32) for i in range(4)]
            t = [pltpu.roll(v, 64, 1) for v in b]
            lhs[rows, 0:128] = jnp.where(low, b[0], t[1]).astype(BF)
            lhs[rows, 128:256] = jnp.where(low, b[2], t[3]).astype(BF)
            if both:
                upper = pl.ds(start + 1024, 128)
                lhs[upper, 0:128] = jnp.where(low, t[0], b[1]).astype(BF)
                lhs[upper, 128:256] = jnp.where(low, t[2], b[3]).astype(BF)
            return carry

        lax.fori_loop(at_row, at_row + count, body, 0)

    bit_of = lax.shift_left(1, lax.broadcasted_iota(jnp.int32, (1, 256), 1) % 8)

    def bits(rows, pair):
        cols = pl.ds(pl.multiple_of(pair * 256, 256), 256)
        byte = jnp.dot(lhs[rows], e[:, cols], preferred_element_type=F32)
        return (byte.astype(jnp.int32) & bit_of) != 0

    def mask_pair(j):
        came(gu.at[pl.ds(2 * j, 2), mine], w_loc.at[j])
        for q in (0, 1):
            keep = bits(slice(q * 1024, (q + 1) * 1024), j)
            cols = slice(q * 128, (q + 1) * 128)
            for i in (0, 1):
                v = gu[2 * j + i, mine, cols].astype(F32)
                v = jnp.where(keep[:, i * 128 : (i + 1) * 128], v, 0.0)
                gu[2 * j + i, mine, cols] = v.astype(BF)

    def swap_pair(j):
        w_remote(2 * j).start()
        w_remote(2 * j + 1).start()

    def mask_and_swap(j, carry):
        mask_pair(j)
        swap_pair(j)
        return carry

    def down_mask(k):
        if k == 0:
            d_words.wait()
            spread_words(0, 14, False)
            dn_local.wait()
        rows = slice(k * 896, (k + 1) * 896)

        def body(j, carry):
            cols = pl.ds(pl.multiple_of(j * 256, 256), 256)
            v = dn[c, rows, cols].astype(F32)
            dn[c, rows, cols] = jnp.where(bits(rows, j), v, 0.0).astype(BF)
            return carry

        lax.fori_loop(0, 4, body, 0)
        dn_remote(k).start()

    def rs_copy(s, d, u):
        return remote(
            rs.at[s, d, u], rs.at[s + 1, d, u], rs_send.at[0], rs_recv.at[s, u],
            at(xs(1 if d == 0 else -1), c, z, y),
        )

    def ag_copy(d, u, hop, block):
        return remote(
            hid.at[d, u, block], hid.at[d, u, block],
            ag_send.at[0], ag_recv.at[u, hop],
            at(xs(1 if d == 0 else -1), c, z, y),
        )

    def product(q, s):
        rows = slice(q * 128, (q + 1) * 128)
        blocks = (xs(-s), xs(s))
        if s == 1:
            came(tok.at[0, 0:192], af_recv.at[q, 1])
        if s == 2:
            came(tok.at[0, 0:96], af_recv.at[q, 0])

        def tile(n, carry):
            if q == 0 and s == 0:
                came(gu.at[0:2, mine], w_recv.at[n])
            for d in (0, 1):
                p[s, d, n] = jnp.dot(
                    tok[blocks[d], rows], gu[d * NT + n], preferred_element_type=F32
                )
            return carry

        lax.fori_loop(0, NT, tile, 0)

    def ring(u, s):
        part = slice((u % 4) * 32, (u % 4) * 32 + 32)
        if s:
            came(rs.at[s, :, u], rs_recv.at[s - 1, u])
        for d in (0, 1):
            if s == 0:
                rs[0, d, u] = p[0, d, :, part].astype(BF)
            elif s < 3:
                rs[s, d, u] = (rs[s, d, u].astype(F32) + p[s, d, :, part]).astype(BF)
            if s < 3:
                rs_copy(s, d, u).start()
                continue
            block = xs(1) if d == 0 else xs(-1)
            for n in range(NT):
                v = rs[3, d, u, n].astype(F32) + p[3, d, n, part]
                gate, up = v[:, :128], v[:, 128:]
                hidden = (gate / (1.0 + jnp.exp(-gate)) * up).astype(BF)
                hid[d, u, block, :, :, n * 128 : (n + 1) * 128] = hidden.reshape(2, 16, 128)
            ag_copy(d, u, 0, block).start()

    def arrived(u, hop):
        came(hid.at[:, u, 0], ag_recv.at[u, hop])
        for d in (0, 1):
            block = xs(-hop) if d == 0 else xs(hop)
            if hop < 2:
                ag_copy(d, u, hop + 1, block).start()

    def squares(q):
        def body(t, carry):
            rows = pl.ds(pl.multiple_of(q * 128 + (t % 4) * 32, 32), 32)
            v = tok[t // 4, rows].astype(F32)
            v = (v * v).reshape(4, 8, FC).sum(axis=0)
            isq[0] += v[:, :1024]
            isq[1] += v[:, 1024:]
            return carry

        lax.fori_loop(0, 16, body, 0)

    def hidden_squares(u):
        def body(t, carry):
            for d in (0, 1):
                v = hid[d, u, t].reshape(32, UH).astype(F32)
                hsq[d] += (v * v).reshape(4, 8, UH).sum(axis=0)
            return carry

        lax.fori_loop(0, NX, body, 0)

    def d_copy(u, i):
        k, h, other = i // 4, (i // 2) % 2, i % 2
        core = lax.rem(c + other, 2)
        block = lax.rem(z + k, 4)
        return remote(
            psend.at[u, core, block, h], drecv.at[u, mp], d_send.at[0], d_recv.at[u],
            at(x, core, block, 2 * c + h),
        )

    def kept_here(i):
        return jnp.logical_and(i // 4 == 0, jnp.logical_and(i % 2 == 0, y == 2 * c + (i // 2) % 2))

    def down(u, count):
        for v in range(u, u + count):
            arrived(v, 2)
        if u == 0:
            came(dn.at[0], dn_recv.at[0])

        def tile(t, carry):
            core, col = t // 2, t % 2
            cols = pl.ds(pl.multiple_of(col * 512, 512), 512)
            acc = sum(
                jnp.dot(
                    hid[d, u : u + count].reshape(count * 128, UH),
                    dn[core, d * UH : (d + 1) * UH, cols],
                    preferred_element_type=F32,
                )
                for d in (0, 1)
            )
            psend[u : u + count, core, :, :, :, cols] = acc.astype(BF).reshape(
                count, NX, 2, 16, 512
            )
            return carry

        lax.fori_loop(0, 4, tile, 0)

        def send(i, carry):
            i = lax.rem(i + 4, 16)
            for v in range(u, u + count):

                @pl.when(jnp.logical_not(kept_here(i)))
                def _():
                    d_copy(v, i).start()

            return carry

        lax.fori_loop(0, 16, send, 0)

        @pl.when(y // 2 == c)
        def _():
            for v in range(u, u + count):
                drecv[v, mp] = psend[v, c, z, y % 2]

        for v in range(u, u + count):
            hidden_squares(v)

    def finish(u):
        here = y // 2 == c

        @pl.when(here)
        def _():
            came(drecv.at[u, 0:15], d_recv.at[u])

        @pl.when(jnp.logical_not(here))
        def _():
            came(drecv.at[u], d_recv.at[u])

        for t in range(2):
            cols = slice(t * 512, (t + 1) * 512)
            total = drecv[u, 0, :, cols].astype(F32)
            for src in range(1, 16):
                total += drecv[u, src, :, cols].astype(F32)
            out[u * 16 : (u + 1) * 16, cols] = total.astype(BF)

    def token_norms():
        copy = remote(isq.at[1 - c], isq_r, n_send.at[0], n_recv.at[0], peer)
        copy.start()
        copy.wait_recv()
        inorm[...] = jnp.sqrt(jnp.sum(isq[c] + isq_r[...], axis=0, keepdims=True))

    def hidden_norms():
        copy = remote(hsq, hsq_r, n_send.at[1], n_recv.at[1], peer)
        copy.start()
        copy.wait_recv()
        for d in (0, 1):
            hnorm[:, d * UH : (d + 1) * UH] = jnp.sqrt(
                jnp.sum(hsq[d] + hsq_r[d], axis=0, keepdims=True)
            )

    tasks = dict(
        product=product, ring=ring, hop=lambda u, h: arrived(u, h - 1), down=down,
        finish=finish, squares=squares, token_norms=token_norms, hidden_norms=hidden_norms,
        down_mask=down_mask,
    )
    tasks["pass"] = pass_on

    with jax.named_scope("words"):
        g_words.wait()
        u_words.wait()
        spread_words(0, 8, True)
        d_words.start()
    with jax.named_scope("norm"):
        norm(0)
        norm(1)
    with jax.named_scope("mask0"):
        mask_pair(0)
    with jax.named_scope("barrier"):
        pl.semaphore_wait(barrier, 34)
    send_tokens(0)
    swap_pair(0)
    send_tokens(1)
    with jax.named_scope("mask"):
        lax.fori_loop(1, NT, mask_and_swap, 0)
    with jax.named_scope("norm"):
        for g in (2, 3):
            norm(g)
            send_tokens(g)
    for task in SCHEDULE:
        with jax.named_scope("_".join(str(v) for v in task)):
            tasks[task[0]](*task[1:])

    with jax.named_scope("sent"):

        came(gu.at[:, mine], w_send.at[0])
        came(dn.at[0], dn_send.at[0])
        came(nsend, ax_send.at[0])
        came(tok.at[0:3, 0:192], af_send.at[0])
        came(rs.at[0:3], rs_send.at[0])
        came(hid.at[:, :, 0:3], ag_send.at[0])
        came(isq.at[0], n_send.at[0])
        came(hsq, n_send.at[1])

        @pl.when(y // 2 == c)
        def _():
            came(drecv.at[:, 0:15], d_send.at[0])

        @pl.when(y // 2 != c)
        def _():
            came(drecv, d_send.at[0])


def main_call(*args):
    dma = pltpu.SemaphoreType.DMA
    vm = pltpu.VMEM
    anywhere = pl.BlockSpec(memory_space=pl.ANY)
    in_vmem = pl.BlockSpec(memory_space=pltpu.VMEM)
    return pl.pallas_call(
        main_kernel,
        in_specs=[anywhere, in_vmem] + [anywhere] * 6,
        out_specs=[in_vmem] * 3,
        out_shape=[
            jax.ShapeDtypeStruct((128, 1024), BF),
            jax.ShapeDtypeStruct((1, 1024), F32),
            jax.ShapeDtypeStruct((1, 1792), F32),
        ],
        scratch_shapes=[
            vm((2 * NT, FC, 256), BF),
            vm((2, 1792, 1024), BF),
            vm((NX, RT, FC), BF),
            vm((4, 2, U, NT, 32, 256), BF),
            vm((2, U, NX, 2, 16, UH), BF),
            vm((4, 2, NT, 128, 256), F32),
            vm((U, 2, NX, 2, 16, 1024), BF),
            vm((U, 16, 16, 1024), BF),
            vm((G, 2, 32, 8192), BF),
            vm((G, 2, 32, 128), F32),
            vm((G, 3, 16, FC), BF),
            vm((128, 1792), jnp.int32),
            vm((2048, 256), BF),
            vm((256, 1792), BF),
            vm((2, 8, 1024), F32),
            vm((8, 1024), F32),
            vm((2, 8, UH), F32),
            vm((2, 8, UH), F32),
            dma((G,)), dma((3,)), dma((NT,)), dma((1,)), dma((NT,)),
            dma((1,)), dma((1,)), dma((1,)),
            dma((1,)), dma((G,)), dma((1,)), dma((2, 2)),
            dma((1,)), dma((3, U)),
            dma((1,)), dma((U, 3)),
            dma((1,)), dma((U,)),
            dma((2,)), dma((2,)),
        ],
        compiler_params=pltpu.CompilerParams(
            collective_id=0, has_side_effects=True, vmem_limit_bytes=67043328
        ),
    )(*args)


def hand_out(mixed, inorm, hnorm, mixed_out, inorm_out, hnorm_out):
    mixed_out[...] = mixed[...]
    inorm_out[...] = inorm[...].reshape(1024)
    hnorm_out[...] = hnorm[...].reshape(1792)


def on_device(
    tokens, norm_gain, gate_weight, gate_mask, up_weight, up_mask, down_weight, down_mask
):
    mixed, inorm, hnorm = main_call(
        tokens, norm_gain.reshape(1, 8192), gate_weight, gate_mask.T, up_weight, up_mask.T,
        down_weight, down_mask.T,
    )
    return pl.pallas_call(
        hand_out,
        out_shape=[
            jax.ShapeDtypeStruct((128, 1024), BF),
            jax.ShapeDtypeStruct((1024,), F32),
            jax.ShapeDtypeStruct((1792,), F32),
        ],
    )(mixed, inorm, hnorm)


def solution(mesh):
    return jax.shard_map(
        on_device,
        mesh=mesh,
        in_specs=(
            P("dp", None), P(), P("dp", "mp"), P("dp", "mp"),
            P("dp", "mp"), P("dp", "mp"), P("mp", "dp"), P("mp", "dp"),
        ),
        out_specs=(P("mp", "dp"), P("dp"), P("mp")),
        check_vma=False,
    )
```

time: 167 us -> 140 us (0.84)
  Pallas kernels: 160 us -> 138 us
  local copies, waits for them, and re-layouts: 2.94 us -> 0 us
    pallas_call x1, Pallas kernels: 160 us -> 136 us  [main_call(): pl.pallas_call(main_kernel, in_specs=[anywhere, in_vmem] + [anywhere] * 6...]
    unnamed x2 -> x0, local copies, waits for them, and re-layouts: 2.94 us -> none
    pallas_call x0 -> x1, Pallas kernels: none -> 1.68 us  [on_device(): pl.pallas_call(hand_out, out_shape=[jax.ShapeDtypeStruct((128, 1024), BF)...]
where the time goes in v3:
time: 140 us; the launch traced here: 138 us
  Pallas kernels  138 us (99%)
    pallas_call x1, Pallas kernels, main_call(): pl.pallas_call(main_kernel, in_specs=[anywhere, in_vmem] + [anywhere] * 6...  136 us

profile of v3, /device:TPU:0, one launch (start us, length us, event | category | flops | bytes accessed | tf_op | source)
XLA Modules:
  0.0 138.5 jit_solution(13010730383382279419)
XLA Ops:
  0.6 136.1 %shard_map.103 = (bf16[128,1024]{1,0:T(8,128)(2,1)}, f32[1,1024]{1,0:T(1,128)}, f32[1,1792]{1,0:T(1,128)}) custom-call(bf16[256,8192]{1,0:T(8,128)(2,1)} %tok_h.1, f32[1,8192]{1,0:T(1,128)} %bitcast.7, bf16[1024,1792]{1,0:T(8,128)(2,1)} %gate_h.1, s32[56,1024]{1,0:T(8,128)} %bitcast.4, bf16[1024,1792]{1,0:T(8,128)(2,1)} %up_h.1, s32[56,1024]{1,0:T(8,128)} %bitcast.5, ...), custom_call_target="tpu_custom_call" | custom-call | tf_op jit(solution)/shard_map/pallas_call | solution.py:480
  136.8 1.7 %shard_map.104 = (bf16[128,1024]{1,0:T(8,128)(2,1)}, f32[1024]{0:T(1024)}, f32[1792]{0:T(1024)}) custom-call(bf16[128,1024]{1,0:T(8,128)(2,1)} %get-tuple-element.6.mixed, f32[1,1024]{1,0:T(1,128)} %get-tuple-element.7.inorm, f32[1,1792]{1,0:T(1,128)} %get-tuple-element.8.hnorm), custom_call_target="tpu_custom_call" | custom-call | tf_op jit(solution)/shard_map/pallas_call | solution.py:535

commit v4 on v3

--- a/solution.py
+++ b/solution.py
@@ -18,22 +18,24 @@
 UH = 896
 
 
+LAST = 7
+
 SCHEDULE = (
-    ("pass", 0), ("pass", 1), ("product", 0, 0), ("ring", 2, 0), ("ring", 0, 0), ("ring", 1, 0),
-    ("ring", 3, 0), ("product", 1, 0), ("ring", 4, 0), ("down_mask", 0), ("pass", 3),
-    ("pass", 2), ("product", 0, 1), ("ring", 0, 1), ("product", 0, 2), ("ring", 2, 1),
-    ("ring", 1, 1), ("ring", 3, 1), ("ring", 0, 2), ("product", 0, 3), ("product", 1, 1),
-    ("ring", 1, 2), ("ring", 0, 3), ("ring", 2, 2), ("ring", 3, 2), ("ring", 1, 3),
-    ("hop", 0, 1), ("product", 1, 2), ("ring", 6, 0), ("ring", 4, 1), ("ring", 7, 0),
-    ("down_mask", 1), ("ring", 3, 3), ("ring", 2, 3), ("squares", 0), ("ring", 4, 2),
-    ("hop", 1, 1), ("product", 1, 3), ("hop", 2, 1), ("hop", 0, 2), ("ring", 4, 3),
-    ("hop", 1, 2), ("ring", 6, 1), ("ring", 7, 1), ("ring", 5, 0), ("down", 0, 2), ("hop", 4, 1),
-    ("hop", 3, 1), ("ring", 5, 1), ("hop", 4, 2), ("ring", 7, 2), ("hop", 2, 2), ("hop", 3, 2),
-    ("ring", 5, 2), ("down", 4, 1), ("ring", 7, 3), ("ring", 6, 2), ("down", 2, 2),
-    ("hop", 7, 1), ("ring", 5, 3), ("ring", 6, 3), ("hop", 7, 2), ("hop", 5, 1), ("hop", 6, 1),
-    ("down", 7, 1), ("hop", 6, 2), ("finish", 0), ("hop", 5, 2), ("down", 6, 1), ("down", 5, 1),
-    ("squares", 1), ("token_norms",), ("finish", 1), ("finish", 6), ("finish", 2), ("finish", 3),
-    ("finish", 7), ("finish", 4), ("hidden_norms",), ("finish", 5),
+    ("pass", 0), ("pass", 1), ("product", 0, 0), ("ring", 0, 0), ("ring", 2, 0), ("ring", 3, 0),
+    ("pass", 2), ("ring", 1, 0), ("product", 1, 0), ("product", 0, 1), ("ring", 0, 1),
+    ("ring", 2, 1), ("down_mask", 0), ("ring", 4, 0), ("pass", 3), ("ring", 1, 1),
+    ("ring", 3, 1), ("product", 0, 3), ("product", 0, 2), ("ring", 2, 2), ("ring", 1, 2),
+    ("product", 1, 1), ("ring", 3, 2), ("ring", 0, 2), ("ring", 2, 3), ("ring", 3, 3),
+    ("ring", 1, 3), ("down_mask", 1), ("ring", 0, 3), ("hop", 2, 1), ("hop", 3, 1),
+    ("hop", 0, 1), ("ring", 6, 0), ("hop", 1, 1), ("hop", 3, 2), ("hop", 2, 2),
+    ("product", 1, 3), ("ring", 4, 1), ("product", 1, 2), ("squares", 0), ("ring", 5, 0), ("ring", 4, 2),
+    ("hop", 0, 2), ("ring", 6, 1), ("down", 2, 2), ("ring", 4, 3), ("hop", 1, 2), ("ring", 5, 1),
+    ("ring", 6, 2), ("ring", 5, 2), ("hop", 4, 1), ("ring", 7, 0), ("down", 0, 2),
+    ("ring", 5, 3), ("hop", 4, 2), ("ring", 6, 3), ("hop", 5, 1), ("ring", 7, 1), ("down", 4, 1),
+    ("hop", 5, 2), ("hop", 6, 1), ("ring", 7, 2), ("down", 5, 1), ("hop", 6, 2), ("ring", 7, 3),
+    ("down", 6, 1), ("squares", 1), ("token_norms",), ("finish", 2), ("finish", 3),
+    ("finish", 0), ("finish", 1), ("finish", 4), ("down", 7, 1), ("finish", 5), ("finish", 6),
+    ("hidden_norms",), ("finish", 7),
 )
 
 
@@ -92,6 +94,20 @@
 
     g_words.start()
     u_words.start()
+
+    barrier = pltpu.get_barrier_semaphore()
+    for k in (1, 2, 3):
+        pl.semaphore_signal(barrier, inc=1, device_id=at(xs(k), c, z, y), device_id_type=MESH)
+
+    def greet(k, carry):
+        other = lax.rem(c * 16 + mp + k, 32)
+        pl.semaphore_signal(
+            barrier, inc=1, device_id=(x * 2 + other // 16, other % 16), device_id_type=MESH
+        )
+        return carry
+
+    lax.fori_loop(1, 32, greet, 0)
+
     for g in (0, 1):
         for h in (0, 1):
             t_local(g, h).start()
@@ -107,22 +123,12 @@
             t_local(g, h).start()
     dn_local.start()
 
-    barrier = pltpu.get_barrier_semaphore()
-    for k in (1, 2, 3):
-        pl.semaphore_signal(barrier, inc=1, device_id=at(xs(k), c, z, y), device_id_type=MESH)
-
-    def greet(k, carry):
-        other = lax.rem(c * 16 + mp + k, 32)
-        pl.semaphore_signal(
-            barrier, inc=1, device_id=(x * 2 + other // 16, other % 16), device_id_type=MESH
-        )
-        return carry
-
-    lax.fori_loop(1, 32, greet, 0)
-
-    k = lax.broadcasted_iota(jnp.int32, (256, 1792), 0)
-    col = lax.broadcasted_iota(jnp.int32, (256, 1792), 1)
-    e[...] = jnp.where((k % 64 == col // 32) & (k // 64 == (col % 32) // 8), 1.0, 0.0).astype(BF)
+    k = lax.broadcasted_iota(jnp.int32, (256, 128), 0)
+    k = (k & 63) * 4 + lax.shift_right_logical(k, 6)
+    for j in range(14):
+        col = lax.broadcasted_iota(jnp.int32, (256, 128), 1) + j * 128
+        here = k == lax.shift_right_logical(col, 3)
+        e[:, j * 128 : (j + 1) * 128] = jnp.where(here, 1.0, 0.0).astype(BF)
     wt[56:64] = jnp.zeros((8, 1792), jnp.int32)
     wt[120:128] = jnp.zeros((8, 1792), jnp.int32)
     wt[32:56, 1024:] = jnp.zeros((24, 768), jnp.int32)
@@ -265,6 +271,11 @@
             at(xs(1 if d == 0 else -1), c, z, y),
         )
 
+    def ag_direct(d, k, block):
+        part = hid.at[d, LAST, block]
+        dev = at(xs(k if d == 0 else -k), c, z, y)
+        return remote(part, part, ag_send.at[0], ag_recv.at[LAST, k - 1], dev)
+
     def product(q, s):
         rows = slice(q * 128, (q + 1) * 128)
         blocks = (xs(-s), xs(s))
@@ -302,7 +313,11 @@
                 gate, up = v[:, :128], v[:, 128:]
                 hidden = (gate / (1.0 + jnp.exp(-gate)) * up).astype(BF)
                 hid[d, u, block, :, :, n * 128 : (n + 1) * 128] = hidden.reshape(2, 16, 128)
-            ag_copy(d, u, 0, block).start()
+            if u == LAST:
+                for k in (2, 1, 3):
+                    ag_direct(d, k, block).start()
+            else:
+                ag_copy(d, u, 0, block).start()
 
     def arrived(u, hop):
         came(hid.at[:, u, 0], ag_recv.at[u, hop])
@@ -343,41 +358,47 @@
     def kept_here(i):
         return jnp.logical_and(i // 4 == 0, jnp.logical_and(i % 2 == 0, y == 2 * c + (i // 2) % 2))
 
+    first_down = next(task for task in SCHEDULE if task[0] == "down")
+
     def down(u, count):
         for v in range(u, u + count):
+            for hop in (0, 1) if v == LAST else ():
+                came(hid.at[:, v, 0], ag_recv.at[v, hop])
             arrived(v, 2)
-        if u == 0:
+        if ("down", u, count) == first_down:
             came(dn.at[0], dn_recv.at[0])
 
-        def tile(t, carry):
-            core, col = t // 2, t % 2
-            cols = pl.ds(pl.multiple_of(col * 512, 512), 512)
-            acc = sum(
-                jnp.dot(
-                    hid[d, u : u + count].reshape(count * 128, UH),
-                    dn[core, d * UH : (d + 1) * UH, cols],
-                    preferred_element_type=F32,
+        for other, core in ((1, 1 - c), (0, c)):
+
+            def tile(t, inner, core=core):
+                cols = pl.ds(pl.multiple_of(t * 512, 512), 512)
+                acc = sum(
+                    jnp.dot(
+                        hid[d, u : u + count].reshape(count * 128, UH),
+                        dn[core, d * UH : (d + 1) * UH, cols],
+                        preferred_element_type=F32,
+                    )
+                    for d in (0, 1)
                 )
-                for d in (0, 1)
-            )
-            psend[u : u + count, core, :, :, :, cols] = acc.astype(BF).reshape(
-                count, NX, 2, 16, 512
-            )
-            return carry
-
-        lax.fori_loop(0, 4, tile, 0)
-
-        def send(i, carry):
-            i = lax.rem(i + 4, 16)
-            for v in range(u, u + count):
-
-                @pl.when(jnp.logical_not(kept_here(i)))
-                def _():
-                    d_copy(v, i).start()
-
-            return carry
-
-        lax.fori_loop(0, 16, send, 0)
+                acc = acc.astype(BF)
+                for i in range(count):
+                    part = acc[i * 128 : (i + 1) * 128].reshape(NX, 2, 16, 512)
+                    psend[u + i, core, :, :, :, cols] = part
+                return inner
+
+            lax.fori_loop(0, 2, tile, 0)
+
+            def send(i, inner, other=other):
+                i = lax.rem(i + 2, 8) * 2 + other
+                for v in range(u, u + count):
+
+                    @pl.when(jnp.logical_not(kept_here(i)))
+                    def _():
+                        d_copy(v, i).start()
+
+                return inner
+
+            lax.fori_loop(0, 8, send, 0)
 
         @pl.when(y // 2 == c)
         def _():

time: 140 us -> 132 us (0.943); the launches traced: 138 us -> 132 us
  Pallas kernels: 138 us -> 132 us
    pallas_call x1, Pallas kernels: 136 us -> 130 us  [main_call(): pl.pallas_call(main_kernel, in_specs=[anywhere, in_vmem] + [anywhere] * 6...]
where the time goes in v4:
time: 132 us
  Pallas kernels  132 us (100%)
    pallas_call x1, Pallas kernels, main_call(): pl.pallas_call(main_kernel, in_specs=[anywhere, in_vmem] + [anywhere] * 6...  130 us

profile of v4, /device:TPU:0, one launch (start us, length us, event | category | flops | bytes accessed | tf_op | source)
XLA Modules:
  0.0 132.3 jit_solution(3826900873849420540)
XLA Ops:
  0.6 130.0 %shard_map.103 = (bf16[128,1024]{1,0:T(8,128)(2,1)}, f32[1,1024]{1,0:T(1,128)}, f32[1,1792]{1,0:T(1,128)}) custom-call(bf16[256,8192]{1,0:T(8,128)(2,1)} %tok_h.1, f32[1,8192]{1,0:T(1,128)} %bitcast.7, bf16[1024,1792]{1,0:T(8,128)(2,1)} %gate_h.1, s32[56,1024]{1,0:T(8,128)} %bitcast.4, bf16[1024,1792]{1,0:T(8,128)(2,1)} %up_h.1, s32[56,1024]{1,0:T(8,128)} %bitcast.5, ...), custom_call_target="tpu_custom_call" | custom-call | tf_op jit(solution)/shard_map/pallas_call | solution.py:501
  130.6 1.7 %shard_map.104 = (bf16[128,1024]{1,0:T(8,128)(2,1)}, f32[1024]{0:T(1024)}, f32[1792]{0:T(1024)}) custom-call(bf16[128,1024]{1,0:T(8,128)(2,1)} %get-tuple-element.6.mixed, f32[1,1024]{1,0:T(1,128)} %get-tuple-element.7.inorm, f32[1,1792]{1,0:T(1,128)} %get-tuple-element.8.hnorm), custom_call_target="tpu_custom_call" | custom-call | tf_op jit(solution)/shard_map/pallas_call | solution.py:556

commit v5 on v4

--- a/solution.py
+++ b/solution.py
@@ -21,29 +21,30 @@
 LAST = 7
 
 SCHEDULE = (
-    ("pass", 0), ("pass", 1), ("product", 0, 0), ("ring", 0, 0), ("ring", 2, 0), ("ring", 3, 0),
-    ("pass", 2), ("ring", 1, 0), ("product", 1, 0), ("product", 0, 1), ("ring", 0, 1),
-    ("ring", 2, 1), ("down_mask", 0), ("ring", 4, 0), ("pass", 3), ("ring", 1, 1),
-    ("ring", 3, 1), ("product", 0, 3), ("product", 0, 2), ("ring", 2, 2), ("ring", 1, 2),
-    ("product", 1, 1), ("ring", 3, 2), ("ring", 0, 2), ("ring", 2, 3), ("ring", 3, 3),
-    ("ring", 1, 3), ("down_mask", 1), ("ring", 0, 3), ("hop", 2, 1), ("hop", 3, 1),
-    ("hop", 0, 1), ("ring", 6, 0), ("hop", 1, 1), ("hop", 3, 2), ("hop", 2, 2),
-    ("product", 1, 3), ("ring", 4, 1), ("product", 1, 2), ("squares", 0), ("ring", 5, 0), ("ring", 4, 2),
-    ("hop", 0, 2), ("ring", 6, 1), ("down", 2, 2), ("ring", 4, 3), ("hop", 1, 2), ("ring", 5, 1),
-    ("ring", 6, 2), ("ring", 5, 2), ("hop", 4, 1), ("ring", 7, 0), ("down", 0, 2),
-    ("ring", 5, 3), ("hop", 4, 2), ("ring", 6, 3), ("hop", 5, 1), ("ring", 7, 1), ("down", 4, 1),
-    ("hop", 5, 2), ("hop", 6, 1), ("ring", 7, 2), ("down", 5, 1), ("hop", 6, 2), ("ring", 7, 3),
-    ("down", 6, 1), ("squares", 1), ("token_norms",), ("finish", 2), ("finish", 3),
-    ("finish", 0), ("finish", 1), ("finish", 4), ("down", 7, 1), ("finish", 5), ("finish", 6),
-    ("hidden_norms",), ("finish", 7),
+    ("pass", 0, 1), ("pass", 1, 1), ("product", 0, 0), ("ring", 0, 0), ("ring", 1, 0),
+    ("pass", 0, 0), ("pass", 1, 0), ("product", 0, 1), ("pass", 2, 1), ("pass", 2, 0),
+    ("ring", 2, 0), ("ring", 3, 0), ("pass", 3, 1), ("pass", 3, 0), ("ring", 1, 1),
+    ("product", 0, 2), ("ring", 2, 1), ("down_mask", 0), ("ring", 0, 1), ("product", 1, 0),
+    ("ring", 1, 2), ("ring", 3, 1), ("product", 0, 3), ("ring", 0, 2), ("ring", 1, 3),
+    ("ring", 3, 2), ("product", 1, 1), ("ring", 0, 3), ("hop", 1, 1), ("ring", 2, 2),
+    ("product", 1, 2), ("squares", 0), ("ring", 4, 0), ("down_mask", 1), ("hop", 1, 2),
+    ("ring", 2, 3), ("hop", 0, 1), ("ring", 3, 3), ("ring", 4, 1), ("product", 1, 3),
+    ("hop", 0, 2), ("ring", 5, 0), ("hop", 2, 1), ("ring", 6, 0), ("hop", 3, 1), ("ring", 4, 2),
+    ("down", 0, 2), ("ring", 5, 1), ("hop", 2, 2), ("hop", 3, 2), ("ring", 4, 3), ("ring", 6, 1),
+    ("ring", 5, 2), ("hop", 4, 1), ("ring", 7, 0), ("down", 2, 2), ("ring", 5, 3), ("hop", 4, 2),
+    ("ring", 6, 2), ("hop", 5, 1), ("ring", 7, 1), ("down", 4, 1), ("ring", 6, 3), ("hop", 5, 2),
+    ("hop", 6, 1), ("ring", 7, 2), ("down", 5, 1), ("hop", 6, 2), ("ring", 7, 3), ("down", 6, 1),
+    ("squares", 1), ("finish", 0), ("finish", 1), ("finish", 2), ("finish", 3), ("finish", 4),
+    ("down", 7, 1), ("finish", 5), ("finish", 6), ("token_norms",), ("hidden_norms",),
+    ("finish", 7),
 )
 
 
 def main_kernel(
-    tok_h, gain, gate_h, gmask_h, up_h, umask_h, dn_h, dmask_h,
+    tok_h, gain_h, gate_h, gmask_h, up_h, umask_h, dn_h, dmask_h,
     out, inorm, hnorm,
     gu, dn, tok, rs, hid, p, psend, drecv, tk, scl, nsend, wt, lhs, e,
-    isq, isq_r, hsq, hsq_r,
+    isq, isq_r, hsq, hsq_r, gain,
     t_sem, m_sem, w_loc, w_send, w_recv, dn_loc, dn_send, dn_recv,
     ax_send, ax_recv, af_send, af_recv, rs_send, rs_recv, ag_send, ag_recv,
     d_send, d_recv, n_send, n_recv,
@@ -86,6 +87,7 @@
     g_words = pltpu.make_async_copy(gmask_h, wt.at[0:56, 0:1024], m_sem.at[0])
     u_words = pltpu.make_async_copy(umask_h, wt.at[64:120, 0:1024], m_sem.at[1])
     d_words = pltpu.make_async_copy(dmask_h, wt.at[0:32], m_sem.at[2])
+    gain_copy = pltpu.make_async_copy(gain_h, gain, m_sem.at[3])
     dn_local = pltpu.make_async_copy(dn_h, dn.at[c], dn_loc.at[0])
 
     def dn_remote(k):
@@ -94,6 +96,7 @@
 
     g_words.start()
     u_words.start()
+    gain_copy.start()
 
     barrier = pltpu.get_barrier_semaphore()
     for k in (1, 2, 3):
@@ -148,7 +151,7 @@
     def ax(g, dx):
         return remote(
             nsend.at[g, dx - 1], tok.at[x, piece(g, coord(g))],
-            ax_send.at[0], ax_recv.at[g], at(xs(dx), c, z, y),
+            ax_send.at[0], ax_recv.at[g, dx % 2], at(xs(dx), c, z, y),
         )
 
     def af(g, dx, dw):
@@ -187,13 +190,13 @@
                 start = g * 64 + i * 32 + h * 16
                 tok[x, start : start + 16] = normed(g, h, slice(i * 16, i * 16 + 16), x)
 
-    def send_tokens(g):
-        for dx in (1, 3, 2):
+    def send_tokens(g, near):
+        for dx in (1, 3) if near else (2,):
             ax(g, dx).start()
 
-    def pass_on(g):
-        came(tok.at[0, 0:48], ax_recv.at[g])
-        for dx in (1, 3, 2):
+    def pass_on(g, near):
+        came(tok.at[0, 0 : 32 if near else 16], ax_recv.at[g, near])
+        for dx in (1, 3) if near else (2,):
             for dw in (1, 3, 2):
                 af(g, dx, dw).start()
 
@@ -204,14 +207,18 @@
             start = pl.multiple_of(r * 128, 128)
             rows = pl.ds(start, 128)
             w = jnp.transpose(wt[:, rows])
-            b = [(lax.shift_right_logical(w, 8 * i) & 255).astype(F32) for i in range(4)]
-            t = [pltpu.roll(v, 64, 1) for v in b]
-            lhs[rows, 0:128] = jnp.where(low, b[0], t[1]).astype(BF)
-            lhs[rows, 128:256] = jnp.where(low, b[2], t[3]).astype(BF)
-            if both:
-                upper = pl.ds(start + 1024, 128)
-                lhs[upper, 0:128] = jnp.where(low, t[0], b[1]).astype(BF)
-                lhs[upper, 128:256] = jnp.where(low, t[2], b[3]).astype(BF)
+            t = pltpu.roll(w, 64, 1)
+
+            def byte_pair(at, below, above, bit):
+                below = lax.shift_right_logical(below, bit)
+                above = lax.shift_right_logical(above, bit + 8)
+                value = jnp.where(low, below, above) & 255
+                lhs[at, bit * 8 : bit * 8 + 128] = value.astype(F32).astype(BF)
+
+            for bit in (0, 16):
+                byte_pair(rows, w, t, bit)
+                if both:
+                    byte_pair(pl.ds(start + 1024, 128), t, w, bit)
             return carry
 
         lax.fori_loop(at_row, at_row + count, body, 0)
@@ -453,22 +460,29 @@
         u_words.wait()
         spread_words(0, 8, True)
         d_words.start()
-    with jax.named_scope("norm"):
-        norm(0)
-        norm(1)
     with jax.named_scope("mask0"):
         mask_pair(0)
     with jax.named_scope("barrier"):
         pl.semaphore_wait(barrier, 34)
-    send_tokens(0)
     swap_pair(0)
-    send_tokens(1)
+    with jax.named_scope("norm"):
+        gain_copy.wait()
+        norm(0)
+        send_tokens(0, 1)
     with jax.named_scope("mask"):
-        lax.fori_loop(1, NT, mask_and_swap, 0)
+        mask_and_swap(1, 0)
+    with jax.named_scope("norm"):
+        norm(1)
+        send_tokens(1, 1)
+        send_tokens(0, 0)
+        send_tokens(1, 0)
+    with jax.named_scope("mask"):
+        lax.fori_loop(2, NT, mask_and_swap, 0)
     with jax.named_scope("norm"):
         for g in (2, 3):
             norm(g)
-            send_tokens(g)
+            send_tokens(g, 1)
+            send_tokens(g, 0)
     for task in SCHEDULE:
         with jax.named_scope("_".join(str(v) for v in task)):
             tasks[task[0]](*task[1:])
@@ -500,7 +514,7 @@
     in_vmem = pl.BlockSpec(memory_space=pltpu.VMEM)
     return pl.pallas_call(
         main_kernel,
-        in_specs=[anywhere, in_vmem] + [anywhere] * 6,
+        in_specs=[anywhere] * 8,
         out_specs=[in_vmem] * 3,
         out_shape=[
             jax.ShapeDtypeStruct((128, 1024), BF),
@@ -526,9 +540,10 @@
             vm((8, 1024), F32),
             vm((2, 8, UH), F32),
             vm((2, 8, UH), F32),
-            dma((G,)), dma((3,)), dma((NT,)), dma((1,)), dma((NT,)),
+            vm((1, 8192), F32),
+            dma((G,)), dma((4,)), dma((NT,)), dma((1,)), dma((NT,)),
             dma((1,)), dma((1,)), dma((1,)),
-            dma((1,)), dma((G,)), dma((1,)), dma((2, 2)),
+            dma((1,)), dma((G, 2)), dma((1,)), dma((2, 2)),
             dma((1,)), dma((3, U)),
             dma((1,)), dma((U, 3)),
             dma((1,)), dma((U,)),

time: 132 us -> 132 us (level)
  no operation moved by 1% of the time
where the time goes in v5:
time: 132 us
  Pallas kernels  131 us (99%)
    pallas_call x1, Pallas kernels, main_call(): pl.pallas_call(main_kernel, in_specs=[anywhere] * 8, out_specs=[in_vmem]...  129 us

profile of v5, /device:TPU:0, one launch (start us, length us, event | category | flops | bytes accessed | tf_op | source)
XLA Modules:
  0.0 131.6 jit_solution(17418049971661173322)
XLA Ops:
  0.6 129.3 %shard_map.103 = (bf16[128,1024]{1,0:T(8,128)(2,1)}, f32[1,1024]{1,0:T(1,128)}, f32[1,1792]{1,0:T(1,128)}) custom-call(bf16[256,8192]{1,0:T(8,128)(2,1)} %tok_h.1, f32[1,8192]{1,0:T(1,128)} %bitcast.7, bf16[1024,1792]{1,0:T(8,128)(2,1)} %gate_h.1, s32[56,1024]{1,0:T(8,128)} %bitcast.4, bf16[1024,1792]{1,0:T(8,128)(2,1)} %up_h.1, s32[56,1024]{1,0:T(8,128)} %bitcast.5, ...), custom_call_target="tpu_custom_call" | custom-call | tf_op jit(solution)/shard_map/pallas_call | solution.py:515
  129.9 1.7 %shard_map.104 = (bf16[128,1024]{1,0:T(8,128)(2,1)}, f32[1024]{0:T(1024)}, f32[1792]{0:T(1024)}) custom-call(bf16[128,1024]{1,0:T(8,128)(2,1)} %get-tuple-element.6.mixed, f32[1,1024]{1,0:T(1,128)} %get-tuple-element.7.inorm, f32[1,1792]{1,0:T(1,128)} %get-tuple-element.8.hnorm), custom_call_target="tpu_custom_call" | custom-call | tf_op jit(solution)/shard_map/pallas_call | solution.py:571

commit v6 on v5

--- a/solution.py
+++ b/solution.py
@@ -21,21 +21,21 @@
 LAST = 7
 
 SCHEDULE = (
-    ("pass", 0, 1), ("pass", 1, 1), ("product", 0, 0), ("ring", 0, 0), ("ring", 1, 0),
-    ("pass", 0, 0), ("pass", 1, 0), ("product", 0, 1), ("pass", 2, 1), ("pass", 2, 0),
-    ("ring", 2, 0), ("ring", 3, 0), ("pass", 3, 1), ("pass", 3, 0), ("ring", 1, 1),
-    ("product", 0, 2), ("ring", 2, 1), ("down_mask", 0), ("ring", 0, 1), ("product", 1, 0),
-    ("ring", 1, 2), ("ring", 3, 1), ("product", 0, 3), ("ring", 0, 2), ("ring", 1, 3),
-    ("ring", 3, 2), ("product", 1, 1), ("ring", 0, 3), ("hop", 1, 1), ("ring", 2, 2),
-    ("product", 1, 2), ("squares", 0), ("ring", 4, 0), ("down_mask", 1), ("hop", 1, 2),
-    ("ring", 2, 3), ("hop", 0, 1), ("ring", 3, 3), ("ring", 4, 1), ("product", 1, 3),
-    ("hop", 0, 2), ("ring", 5, 0), ("hop", 2, 1), ("ring", 6, 0), ("hop", 3, 1), ("ring", 4, 2),
-    ("down", 0, 2), ("ring", 5, 1), ("hop", 2, 2), ("hop", 3, 2), ("ring", 4, 3), ("ring", 6, 1),
-    ("ring", 5, 2), ("hop", 4, 1), ("ring", 7, 0), ("down", 2, 2), ("ring", 5, 3), ("hop", 4, 2),
-    ("ring", 6, 2), ("hop", 5, 1), ("ring", 7, 1), ("down", 4, 1), ("ring", 6, 3), ("hop", 5, 2),
-    ("hop", 6, 1), ("ring", 7, 2), ("down", 5, 1), ("hop", 6, 2), ("ring", 7, 3), ("down", 6, 1),
+    ("pass", 0, 1), ("pass", 1, 1), ("product", 0, 0), ("ring", 2, 0), ("ring", 0, 0),
+    ("ring", 1, 0), ("ring", 3, 0), ("pass", 0, 0), ("pass", 1, 0), ("product", 0, 1),
+    ("pass", 3, 1), ("pass", 3, 0), ("down_mask", 0), ("ring", 0, 1), ("ring", 1, 1),
+    ("ring", 3, 1), ("pass", 2, 1), ("pass", 2, 0), ("product", 0, 2), ("ring", 0, 2),
+    ("ring", 1, 2), ("ring", 2, 1), ("product", 0, 3), ("product", 1, 0), ("ring", 3, 2),
+    ("ring", 1, 3), ("ring", 2, 2), ("ring", 0, 3), ("product", 1, 1), ("ring", 3, 3),
+    ("down_mask", 1), ("ring", 4, 0), ("hop", 1, 1), ("hop", 0, 1), ("ring", 2, 3),
+    ("ring", 4, 1), ("hop", 1, 2), ("hop", 0, 2), ("hop", 2, 1), ("ring", 6, 0), ("hop", 3, 1),
+    ("product", 1, 3), ("product", 1, 2), ("squares", 0), ("ring", 4, 2), ("ring", 5, 0),
+    ("down", 0, 2), ("hop", 3, 2), ("ring", 6, 1), ("ring", 4, 3), ("hop", 2, 2), ("ring", 5, 1),
+    ("ring", 6, 2), ("hop", 4, 1), ("ring", 7, 0), ("down", 2, 2), ("ring", 6, 3), ("hop", 4, 2),
+    ("ring", 5, 2), ("hop", 6, 1), ("ring", 7, 1), ("down", 4, 1), ("ring", 5, 3), ("hop", 6, 2),
+    ("hop", 5, 1), ("ring", 7, 2), ("down", 6, 1), ("hop", 5, 2), ("ring", 7, 3), ("down", 5, 1),
     ("squares", 1), ("finish", 0), ("finish", 1), ("finish", 2), ("finish", 3), ("finish", 4),
-    ("down", 7, 1), ("finish", 5), ("finish", 6), ("token_norms",), ("hidden_norms",),
+    ("down", 7, 1), ("finish", 6), ("finish", 5), ("token_norms",), ("hidden_norms",),
     ("finish", 7),
 )
 

time: 132 us -> 130 us (0.985)
    pallas_call x1, Pallas kernels: 129 us -> 128 us  [main_call(): pl.pallas_call(main_kernel, in_specs=[anywhere] * 8, out_specs=[in_vmem]...]
where the time goes in v6:
time: 130 us
  Pallas kernels  130 us (100%)
    pallas_call x1, Pallas kernels, main_call(): pl.pallas_call(main_kernel, in_specs=[anywhere] * 8, out_specs=[in_vmem]...  128 us

profile of v6, /device:TPU:0, one launch (start us, length us, event | category | flops | bytes accessed | tf_op | source)
XLA Modules:
  0.0 130.3 jit_solution(10892443320474246625)
XLA Ops:
  0.6 128.0 %shard_map.103 = (bf16[128,1024]{1,0:T(8,128)(2,1)}, f32[1,1024]{1,0:T(1,128)}, f32[1,1792]{1,0:T(1,128)}) custom-call(bf16[256,8192]{1,0:T(8,128)(2,1)} %tok_h.1, f32[1,8192]{1,0:T(1,128)} %bitcast.7, bf16[1024,1792]{1,0:T(8,128)(2,1)} %gate_h.1, s32[56,1024]{1,0:T(8,128)} %bitcast.4, bf16[1024,1792]{1,0:T(8,128)(2,1)} %up_h.1, s32[56,1024]{1,0:T(8,128)} %bitcast.5, ...), custom_call_target="tpu_custom_call" | custom-call | tf_op jit(solution)/shard_map/pallas_call | solution.py:515
  128.6 1.7 %shard_map.104 = (bf16[128,1024]{1,0:T(8,128)(2,1)}, f32[1024]{0:T(1024)}, f32[1792]{0:T(1024)}) custom-call(bf16[128,1024]{1,0:T(8,128)(2,1)} %get-tuple-element.6.mixed, f32[1,1024]{1,0:T(1,128)} %get-tuple-element.7.inorm, f32[1,1792]{1,0:T(1,128)} %get-tuple-element.8.hnorm), custom_call_target="tpu_custom_call" | custom-call | tf_op jit(solution)/shard_map/pallas_call | solution.py:571
